TPU v7x, 32 devices: a 4x4x1 block of a 4x4x8 slice. The times are simulated.
32 devices in a mesh: rep: 2 (over z, core), dp: 16 (over x, y).
Axes of the slice: x: 4, y: 4, z: 1, core: 2. Of those that a mesh axis runs over, the one named last changes fastest.
The devices are a block of a 4x4x8 slice.
Arguments:
- x: bfloat16 [32, 4096, 896], P(('rep', 'dp')), parts along dimension 0
- dy: bfloat16 [32, 4096, 896], P(('rep', 'dp')), parts along dimension 0
- w_gate: bfloat16 [2, 896, 2560], P(None, 'dp')
- w_up: bfloat16 [2, 896, 2560], P(None, 'dp')
- w_down: bfloat16 [2, 2560, 896], P(None, 'dp')
- m_w_gate: float32 [2, 896, 2560], P(None, 'dp')
- m_w_up: float32 [2, 896, 2560], P(None, 'dp')
- m_w_down: float32 [2, 2560, 896], P(None, 'dp')
- v_w_gate: float32 [2, 896, 2560], P(None, 'dp')
- v_w_up: float32 [2, 896, 2560], P(None, 'dp')
- v_w_down: float32 [2, 2560, 896], P(None, 'dp')
Outputs:
- output 1: bfloat16 [4, 896, 2560], P('rep', 'dp'), parts along dimension 0
- output 2: bfloat16 [4, 896, 2560], P('rep', 'dp'), parts along dimension 0
- output 3: bfloat16 [4, 2560, 896], P('rep', 'dp'), parts along dimension 0
- output 4: float32 [4, 896, 2560], P('rep', 'dp'), parts along dimension 0
- output 5: float32 [4, 896, 2560], P('rep', 'dp'), parts along dimension 0
- output 6: float32 [4, 2560, 896], P('rep', 'dp'), parts along dimension 0
- output 7: float32 [4, 896, 2560], P('rep', 'dp'), parts along dimension 0
- output 8: float32 [4, 896, 2560], P('rep', 'dp'), parts along dimension 0
- output 9: float32 [4, 2560, 896], P('rep', 'dp'), parts along dimension 0
There are 2 independent parts. A program takes and returns all parts, laid end to end along the dimension named above; an argument that names none is the same for every part.
All inputs are finite; a program needn't handle non-finite values.
Results may differ from a plain program's by a relative error of at most 0.022.
Values are sent between devices in bfloat16 or wider.
A program may use at most 768 MiB of HBM per device.

v0:
```python
import jax
import jax.numpy as jnp
from jax import lax
from jax.sharding import PartitionSpec as P

NAMES = ("w_gate", "w_up", "w_down")


def matmul(a, w):
    return jnp.dot(a, w, preferred_element_type=jnp.float32).astype(jnp.bfloat16)


def normed(h):
    wide = h.astype(jnp.float32)
    scale = lax.rsqrt(jnp.mean(wide**2, -1, keepdims=True) + 1e-6)
    return (wide * scale).astype(jnp.bfloat16)


def layer(h, w):
    a = normed(h)
    gate = jnp.dot(a, w["w_gate"], preferred_element_type=jnp.float32)
    up = jnp.dot(a, w["w_up"], preferred_element_type=jnp.float32)
    return h + matmul((jax.nn.silu(gate) * up).astype(jnp.bfloat16), w["w_down"])


def adamw(w, m, v, g):
    m = 0.9 * m + 0.1 * g
    v = 0.95 * v + 0.05 * g * g
    step = m * lax.rsqrt(v + 1e-8) + 0.1 * w
    return (w - 0.02 * step).astype(jnp.bfloat16), m, v


def clipped(gradients, sum_of_squares, count):
    factor = jnp.minimum(1.0, 0.5 * lax.rsqrt(sum_of_squares / count + 1e-30))
    return [g * factor for g in gradients]


def solution(mesh):
    def fetched(weights, number):
        return {name: lax.all_gather(w[number], "dp", axis=0, tiled=True) for name, w in zip(NAMES, weights, strict=True)}

    def step(x, dy, *arrays):
        weights, m, v = (arrays[i : i + 3] for i in (0, 3, 6))
        layers = weights[0].shape[0]
        h, kept = x[0], []
        for number in range(layers):
            kept.append(h)
            h = layer(h, fetched(weights, number))
        by_h, mine = dy[0], [None] * layers
        for number in reversed(range(layers)):
            _, back = jax.vjp(lambda w, h: layer(h, w), fetched(weights, number), kept[number])
            by_w, by_h = back(by_h)
            mine[number] = [lax.psum_scatter(by_w[name], "dp", scatter_dimension=0, tiled=True) for name in NAMES]
        gradients = [jnp.stack([mine[number][i] for number in range(layers)]).astype(jnp.float32) for i in range(3)]
        squares = lax.psum(sum(jnp.sum(g * g) for g in gradients), "dp")
        gradients = clipped(gradients, squares, lax.psum(1, "dp") * sum(g.size for g in gradients))
        new = [adamw(w.astype(jnp.float32), m, v, g) for w, m, v, g in zip(weights, m, v, gradients, strict=True)]
        return tuple(one[which] for which in range(3) for one in new)

    states, cut = P(("rep", "dp"), None, None), P(None, "dp", None)
    return jax.shard_map(
        step,
        mesh=mesh,
        in_specs=(states, states) + (cut,) * 9,
        out_specs=(P("rep", "dp", None),) * 9,
        check_vma=False,
    )
```

profile of v0, /device:TPU:96, one launch (start us, length us, event | category | flops | bytes accessed | tf_op | source)
XLA Modules:
  0.0 985.6 jit_solution(9637303911967005181)
XLA Ops:
  7.3 1.9 fusion.91
  9.2 0.1 all-gather.15.cloned.1.call-start
  9.3 1.9 fusion.90
  11.3 1.9 fusion.89
  13.3 0.6 all-gather.23.cloned.1.call-update
  14.0 0.6 all-gather.21.cloned.1.call-update
  14.6 0.6 all-gather.19.cloned.1.call-update
  15.3 10.8 %copy.22 = bf16[1,4096,896]{1,2,0:T(8,128)(2,1)} copy(bf16[1,4096,896]{2,1,0:T(8,128)(2,1)} %param.11) | data formatting | bytes 14680064 | tf_op args[0]
  26.0 4.6 fusion.15
  30.6 10.7 %copy.23 = bf16[1,4096,896]{1,2,0:T(8,128)(2,1)} copy(bf16[1,4096,896]{2,1,0:T(8,128)(2,1)} %param.12) | data formatting | bytes 14680064 | tf_op args[1]
  41.3 19.6 %all-gather.13.cloned.1.call-done = bf16[1,896,2560]{2,1,0:T(8,128)(2,1)} async-done(((bf16[1,56,2560]{2,1,0:T(8,128)(2,1)}), bf16[1,896,2560]{2,1,0:T(8,128)(2,1)}) %all-gather.13.cloned.1.call-update) | async-done | bytes 4587536 | tf_op jit(solution)/shard_map/all_gather | solution.py:40
  61.0 29.4 %fusion.44 = f32[4096,2560]{1,0:T(8,128)} fusion(bf16[1,4096,896]{1,2,0:T(8,128)(2,1)} %copy.22, f32[4096]{0:T(1024)S(1)} %add_rsqrt_fusion, bf16[1,896,2560]{2,1,0:T(8,128)(2,1)} %all-gather.13.cloned.1.call-done), kind=kOutput, calls=%fused_computation.54 | convolution fusion | flops 18801491968 | bytes 53886976 | tf_op jit(solution)/shard_map/dot_general | solution.py:21
  90.4 20.6 %all-gather.15.cloned.1.call-done = bf16[1,896,2560]{2,1,0:T(8,128)(2,1)} async-done(((bf16[1,56,2560]{2,1,0:T(8,128)(2,1)}), bf16[1,896,2560]{2,1,0:T(8,128)(2,1)}) %all-gather.15.cloned.1.call-update) | async-done | bytes 4587536 | tf_op jit(solution)/shard_map/all_gather | solution.py:40
  111.0 49.7 %multiply_convert_fusion.1 = (bf16[4096,2560]{1,0:T(8,128)(2,1)}, f32[4096,2560]{1,0:T(8,128)}) fusion(f32[4096,2560]{1,0:T(8,128)} %fusion.44, bf16[1,896,2560]{2,1,0:T(8,128)(2,1)} %all-gather.15.cloned.1.call-done, bf16[1,4096,896]{1,2,0:T(8,128)(2,1)} %copy.22, f32[4096]{0:T(1024)S(1)} %add_rsqrt_fusion), kind=kOutput, calls=%fused_computation.17 | convolution fusion | flops 18864406528 | bytes 116801536 | tf_op jit(solution)/shard_map/dot_general | solution.py:22
  160.7 0.4 all-gather.17.cloned.1.call-done
  161.1 26.8 %fusion.19 = (f32[4096]{0:T(1024)S(1)}, bf16[4096,896]{0,1:T(8,128)(2,1)}) fusion(bf16[4096,2560]{1,0:T(8,128)(2,1)} %get-tuple-element.24, bf16[1,2560,896]{2,1,0:T(8,128)(2,1)} %all-gather.17.cloned.1.call-done, bf16[1,4096,896]{1,2,0:T(8,128)(2,1)} %copy.22), kind=kOutput, calls=%fused_computation.37 | convolution fusion | flops 18808827904 | bytes 40255488 | tf_op jit(solution)/shard_map/dot_general | solution.py:10
  187.9 0.6 copy-done.9
  188.5 22.4 %all-gather.23.cloned.1.call-done = bf16[1,896,2560]{2,1,0:T(8,128)(2,1)} async-done(((bf16[1,56,2560]{2,1,0:T(8,128)(2,1)}), bf16[1,896,2560]{2,1,0:T(8,128)(2,1)}) %all-gather.23.cloned.1.call-update) | async-done | bytes 4587536 | tf_op jit(solution)/shard_map/all_gather | solution.py:40
  211.0 29.6 %fusion.36 = f32[4096,2560]{1,0:T(8,128)} fusion(bf16[4096,896]{0,1:T(8,128)(2,1)} %get-tuple-element.27, f32[4096]{0:T(1024)S(1)} %fusion.77, bf16[1,896,2560]{2,1,0:T(8,128)(2,1)} %all-gather.23.cloned.1.call-done), kind=kOutput, calls=%fused_computation.51 | convolution fusion | flops 18801491968 | bytes 53886976 | tf_op jit(solution)/shard_map/jvp()/dot_general | solution.py:22
  240.6 20.3 %all-gather.21.cloned.1.call-done = bf16[1,2560,896]{2,1,0:T(8,128)(2,1)} async-done(((bf16[1,160,896]{2,1,0:T(8,128)(2,1)}), bf16[1,2560,896]{2,1,0:T(8,128)(2,1)}) %all-gather.21.cloned.1.call-update) | async-done | bytes 4587536 | tf_op jit(solution)/shard_map/all_gather | solution.py:40
  260.8 28.4 %convolution_convert_fusion.1 = bf16[4096,2560]{1,0:T(8,128)(2,1)} fusion(bf16[1,4096,896]{2,1,0:T(8,128)(2,1)} %param.12, bf16[1,2560,896]{2,1,0:T(8,128)(2,1)} %all-gather.21.cloned.1.call-done), kind=kOutput, calls=%fused_computation.27 | convolution fusion | flops 18800967680 | bytes 32899072 | tf_op jit(solution)/shard_map/transpose(jvp())/dot_general | solution.py:10
  289.3 21.5 %all-gather.19.cloned.1.call-done = bf16[1,896,2560]{2,1,0:T(8,128)(2,1)} async-done(((bf16[1,56,2560]{2,1,0:T(8,128)(2,1)}), bf16[1,896,2560]{2,1,0:T(8,128)(2,1)}) %all-gather.19.cloned.1.call-update) | async-done | bytes 4587536 | tf_op jit(solution)/shard_map/all_gather | solution.py:40
  310.7 58.3 %fusion.2 = (bf16[4096,2560]{1,0:T(8,128)(2,1)}, f32[4096,2560]{1,0:T(8,128)}) fusion(f32[4096,2560]{1,0:T(8,128)} %fusion.36, bf16[4096,2560]{1,0:T(8,128)(2,1)} %convolution_convert_fusion.1, bf16[1,896,2560]{2,1,0:T(8,128)(2,1)} %all-gather.19.cloned.1.call-done, bf16[4096,896]{0,1:T(8,128)(2,1)} %get-tuple-element.27, f32[4096]{0:T(1024)S(1)} %fusion.77), kind=kOutput, calls=%fused_computation.8 | convolution fusion | flops 18927321088 | bytes 137773056 | tf_op jit(solution)/shard_map/jvp()/dot_general | solution.py:21
  369.1 23.6 %fusion.49 = bf16[4096,896]{0,1:T(8,128)(2,1)} fusion(bf16[4096,2560]{1,0:T(8,128)(2,1)} %get-tuple-element.28, bf16[1,896,2560]{2,1,0:T(8,128)(2,1)S(1)} %copy-done.13), kind=kOutput, calls=%fused_computation.58 | convolution fusion | flops 18790481920 | bytes 32899072 | tf_op jit(solution)/shard_map/transpose(jvp())/dot_general | solution.py:21
  392.7 38.7 %fusion.21 = (f32[4096]{0:T(1024)S(1)}, bf16[4096,896]{0,1:T(8,128)(2,1)}) fusion(bf16[4096,896]{0,1:T(8,128)(2,1)} %get-tuple-element.27, bf16[4096,896]{0,1:T(8,128)(2,1)} %fusion.49, bf16[1,896,2560]{2,1,0:T(8,128)(2,1)} %all-gather.23.cloned.1.call-done, bf16[4096,2560]{1,0:T(8,128)(2,1)} %convolution_convert_fusion.1, f32[4096,2560]{1,0:T(8,128)} %get-tuple-element.29), kind=kOutput, calls=%fused_computation.39 | convolution fusion | flops 18875412480 | bytes 89538560 | tf_op jit(solution)/shard_map/transpose(jvp())/dot_general | solution.py:22
  431.4 9.8 fusion.22
  441.2 3.0 copy-done
  444.2 26.4 %convolution_convert_fusion.2 = bf16[2560,896]{1,0:T(8,128)(2,1)} fusion(bf16[4096,2560]{1,0:T(8,128)(2,1)} %get-tuple-element.24, bf16[4096,896]{0,1:T(8,128)(2,1)S(1)} %fusion.22), kind=kOutput, calls=%fused_computation.49 | convolution fusion | flops 18792775680 | bytes 32899072 | tf_op jit(solution)/shard_map/transpose(jvp())/dot_general | solution.py:10
  470.7 0.5 reduce-scatter.17.cloned.1.call-start
  471.1 35.7 %fusion.26 = bf16[2560,896]{1,0:T(8,128)(2,1)} fusion(bf16[1,4096,896]{2,1,0:T(8,128)(2,1)} %param.12, f32[4096,2560]{1,0:T(8,128)} %fusion.36, f32[4096,2560]{1,0:T(8,128)} %get-tuple-element.29), kind=kOutput, calls=%fused_computation.45 | convolution fusion | flops 18855690240 | bytes 95813632 | tf_op jit(solution)/shard_map/transpose(jvp())/dot_general | solution.py:10
  506.9 0.1 reduce-scatter.23.cloned.1.call-start
  507.0 27.7 %convolution_convert_fusion = bf16[4096,2560]{1,0:T(8,128)(2,1)} fusion(bf16[4096,896]{0,1:T(8,128)(2,1)} %copy-done, bf16[1,2560,896]{2,1,0:T(8,128)(2,1)} %all-gather.17.cloned.1.call-done), kind=kOutput, calls=%fused_computation.26 | convolution fusion | flops 18800967680 | bytes 32899072 | tf_op jit(solution)/shard_map/transpose(jvp())/dot_general | solution.py:10
  534.7 34.2 %fusion.33 = bf16[896,2560]{1,0:T(8,128)(2,1)} fusion(bf16[4096,2560]{1,0:T(8,128)(2,1)} %convolution_convert_fusion, f32[4096,2560]{1,0:T(8,128)} %fusion.44, bf16[1,4096,896]{1,2,0:T(8,128)(2,1)} %copy.22, f32[4096]{0:T(1024)S(1)} %copy-done.12), kind=kOutput, calls=%fused_computation.48 | convolution fusion | flops 18866700288 | bytes 74858496 | tf_op jit(solution)/shard_map/transpose(jvp())/dot_general | solution.py:22
  569.0 0.2 reduce-scatter.25.cloned.1.call-start
  569.2 34.1 %fusion.29 = bf16[896,2560]{1,0:T(8,128)(2,1)} fusion(bf16[4096,2560]{1,0:T(8,128)(2,1)} %convolution_convert_fusion.1, bf16[4096,896]{0,1:T(8,128)(2,1)} %get-tuple-element.27, f32[4096]{0:T(1024)S(1)} %copy-done.8, f32[4096,2560]{1,0:T(8,128)} %get-tuple-element.29), kind=kOutput, calls=%fused_computation.46 | convolution fusion | flops 18866700288 | bytes 74858496 | tf_op jit(solution)/shard_map/transpose(jvp())/dot_general | solution.py:22
  603.4 42.1 %fusion.30 = bf16[896,2560]{1,0:T(8,128)(2,1)} fusion(f32[4096,2560]{1,0:T(8,128)} %fusion.44, f32[4096,2560]{1,0:T(8,128)} %get-tuple-element.25, bf16[4096,2560]{1,0:T(8,128)(2,1)} %convolution_convert_fusion, bf16[1,4096,896]{1,2,0:T(8,128)(2,1)} %copy.22, f32[4096]{0:T(1024)S(1)} %copy-done.12), kind=kOutput, calls=%fused_computation.47 | convolution fusion | flops 18919129088 | bytes 116801536 | tf_op jit(solution)/shard_map/transpose(jvp())/dot_general | solution.py:21
  645.6 0.3 reduce-scatter.21.cloned.1.call-start
  645.9 25.3 %convolution_convert_fusion.3 = bf16[896,2560]{1,0:T(8,128)(2,1)} fusion(bf16[4096,2560]{1,0:T(8,128)(2,1)} %get-tuple-element.28, bf16[4096,896]{0,1:T(8,128)(2,1)} %get-tuple-element.27, f32[4096]{0:T(1024)S(1)} %copy-done.8), kind=kOutput, calls=%fused_computation.50 | convolution fusion | flops 18801491968 | bytes 32915456 | tf_op jit(solution)/shard_map/transpose(jvp())/dot_general | solution.py:21
  671.4 2.0 fusion.67
  673.4 23.9 %reduce-scatter.23.cloned.1.call-done = bf16[56,2560]{1,0:T(8,128)(2,1)} async-done(((bf16[896,2560]{1,0:T(8,128)(2,1)}), bf16[56,2560]{1,0:T(8,128)(2,1)}) %reduce-scatter.23.cloned.1.call-update) | async-done | bytes 286736
  697.3 76.1 %reduce-scatter.25.cloned.1.call-done = bf16[56,2560]{1,0:T(8,128)(2,1)} async-done(((bf16[896,2560]{1,0:T(8,128)(2,1)}), bf16[56,2560]{1,0:T(8,128)(2,1)}) %reduce-scatter.25.cloned.1.call-update) | async-done | bytes 286736
  773.5 2.0 fusion.66
  775.4 74.5 %reduce-scatter.19.cloned.1.call-done = bf16[56,2560]{1,0:T(8,128)(2,1)} async-done(((bf16[896,2560]{1,0:T(8,128)(2,1)}), bf16[56,2560]{1,0:T(8,128)(2,1)}) %reduce-scatter.19.cloned.1.call-update) | async-done | bytes 286736
  850.0 76.2 %reduce-scatter.21.cloned.1.call-done = bf16[56,2560]{1,0:T(8,128)(2,1)} async-done(((bf16[896,2560]{1,0:T(8,128)(2,1)}), bf16[56,2560]{1,0:T(8,128)(2,1)}) %reduce-scatter.21.cloned.1.call-update) | async-done | bytes 286736
  926.2 1.9 fusion.65
  930.1 38.7 %psum.7 = f32[]{:T(128)} all-reduce(f32[]{:T(128)S(6)} %add.99), channel_id=1, replica_groups=mesh['rep'=2,'dp'=16] {'dp'}, use_global_device_ids=true, to_apply=%region_12.13 | all-reduce | flops 1 | bytes 8 | tf_op jit(solution)/shard_map/psum | solution.py:55
  969.5 3.3 fusion.73
  972.8 5.7 fusion.64
  (47 shorter events, 1.1 us)
Async XLA Ops:
  7.2 53.8 %all-gather.13.cloned.1.call-start = ((), (), s32[]{:S(2)}) async-start(), calls=%async_computation.8 | async-start | bytes 4874240 | tf_op jit(solution)/shard_map/all_gather | solution.py:40
  9.2 101.8 %all-gather.15.cloned.1.call-start = ((), (), s32[]{:S(2)}) async-start(), calls=%async_computation.9 | async-start | bytes 4874240 | tf_op jit(solution)/shard_map/all_gather | solution.py:40
  11.2 149.8 %all-gather.17.cloned.1.call-start = ((), (), s32[]{:S(2)}) async-start(), calls=%async_computation.10 | async-start | bytes 4874240 | tf_op jit(solution)/shard_map/all_gather | solution.py:40
  13.3 197.7 %all-gather.23.cloned.1.call-start = ((), (), s32[]{:S(2)}) async-start(), calls=%async_computation.13 | async-start | bytes 4874240 | tf_op jit(solution)/shard_map/all_gather | solution.py:40
  13.9 246.9 %all-gather.21.cloned.1.call-start = ((), (), s32[]{:S(2)}) async-start(), calls=%async_computation.12 | async-start | bytes 4874240 | tf_op jit(solution)/shard_map/all_gather | solution.py:40
  14.6 296.2 %all-gather.19.cloned.1.call-start = ((), (), s32[]{:S(2)}) async-start(), calls=%async_computation.11 | async-start | bytes 4874240 | tf_op jit(solution)/shard_map/all_gather | solution.py:40
  15.2 656.1 %reduce-scatter.15.cloned.1.call-start = ((), (), s32[]{:S(2)}) async-start(), calls=%async_computation.6 | async-start | bytes 4874240 | tf_op jit(solution)/shard_map/reduce_scatter | solution.py:53
  30.6 80.4 %copy-start.11 = (f32[4096]{0:T(1024)}, f32[4096]{0:T(1024)S(1)}, u32[]{:S(2)}) copy-start(f32[4096]{0:T(1024)S(1)} %add_rsqrt_fusion) | copy-start | bytes 49156
  187.9 0.6 copy-start.9
  188.5 242.9 %copy-start.7 = (f32[4096]{0:T(1024)}, f32[4096]{0:T(1024)S(1)}, u32[]{:S(2)}) copy-start(f32[4096]{0:T(1024)S(1)} %fusion.77) | copy-start | bytes 49156
  310.7 58.4 %copy-start.13 = (bf16[1,896,2560]{2,1,0:T(8,128)(2,1)S(1)}, bf16[1,896,2560]{2,1,0:T(8,128)(2,1)}, u32[]{:S(2)}) copy-start(bf16[1,896,2560]{2,1,0:T(8,128)(2,1)} %all-gather.19.cloned.1.call-done) | copy-start | bytes 13762564
  392.7 38.7 %copy-start.10 = (f32[4096]{0:T(1024)S(1)}, f32[4096]{0:T(1024)}, u32[]{:S(2)}) copy-start(f32[4096]{0:T(1024)} %copy-done.9) | copy-start | bytes 49156
  441.2 3.0 copy-start
  470.7 200.7 %reduce-scatter.17.cloned.1.call-start = ((), (), s32[]{:S(2)}) async-start(), calls=%async_computation.7 | async-start | bytes 4874240 | tf_op jit(solution)/shard_map/reduce_scatter | solution.py:53
  506.9 27.8 %copy-start.12 = (f32[4096]{0:T(1024)S(1)}, f32[4096]{0:T(1024)}, u32[]{:S(2)}) copy-start(f32[4096]{0:T(1024)} %copy-done.11) | copy-start | bytes 49156
  506.9 190.4 %reduce-scatter.23.cloned.1.call-start = ((), (), s32[]{:S(2)}) async-start(), calls=%async_computation.16 | async-start | bytes 4874240
  534.7 34.5 %copy-start.8 = (f32[4096]{0:T(1024)S(1)}, f32[4096]{0:T(1024)}, u32[]{:S(2)}) copy-start(f32[4096]{0:T(1024)} %copy-done.7) | copy-start | bytes 49156
  569.0 204.5 %reduce-scatter.25.cloned.1.call-start = ((), (), s32[]{:S(2)}) async-start(), calls=%async_computation.17 | async-start | bytes 4874240
  603.4 246.6 %reduce-scatter.19.cloned.1.call-start = ((), (), s32[]{:S(2)}) async-start(), calls=%async_computation.14 | async-start | bytes 4874240
  645.6 323.9 %copy-start.1 = (bf16[2,160,896]{2,1,0:T(8,128)(2,1)S(1)}, bf16[2,160,896]{2,1,0:T(8,128)(2,1)}, u32[]{:S(2)}) copy-start(bf16[2,160,896]{2,1,0:T(8,128)(2,1)} %param.15) | copy-start | bytes 1720324
  645.6 323.9 %copy-start.4 = (f32[2,160,896]{2,1,0:T(8,128)S(1)}, f32[2,160,896]{2,1,0:T(8,128)}, u32[]{:S(2)}) copy-start(f32[2,160,896]{2,1,0:T(8,128)} %param.21) | copy-start | bytes 3440644
  645.6 280.6 %reduce-scatter.21.cloned.1.call-start = ((), (), s32[]{:S(2)}) async-start(), calls=%async_computation.15 | async-start | bytes 4874240
  671.2 301.6 %copy-start.2 = (bf16[2,56,2560]{2,1,0:T(8,128)(2,1)S(1)}, bf16[2,56,2560]{2,1,0:T(8,128)(2,1)}, u32[]{:S(2)}) copy-start(bf16[2,56,2560]{2,1,0:T(8,128)(2,1)} %param.13) | copy-start | bytes 1720324
  671.2 301.6 %copy-start.3 = (bf16[2,56,2560]{2,1,0:T(8,128)(2,1)S(1)}, bf16[2,56,2560]{2,1,0:T(8,128)(2,1)}, u32[]{:S(2)}) copy-start(bf16[2,56,2560]{2,1,0:T(8,128)(2,1)} %param.14) | copy-start | bytes 1720324
  697.3 275.5 %copy-start.5 = (bf16[56,2560]{1,0:T(8,128)(2,1)S(1)}, bf16[56,2560]{1,0:T(8,128)(2,1)}, u32[]{:S(2)}) copy-start(bf16[56,2560]{1,0:T(8,128)(2,1)} %reduce-scatter.23.cloned.1.call-done) | copy-start | bytes 860164
  773.5 199.4 %copy-start.6 = (bf16[56,2560]{1,0:T(8,128)(2,1)S(1)}, bf16[56,2560]{1,0:T(8,128)(2,1)}, u32[]{:S(2)}) copy-start(bf16[56,2560]{1,0:T(8,128)(2,1)} %reduce-scatter.25.cloned.1.call-done) | copy-start | bytes 860164
Sparse Core Ops, SparseCore 0:
  10.6 50.3 all-gather.12
  63.5 47.4 all-gather.14
  113.6 47.4 all-gather.16
  163.5 47.4 all-gather.22
  213.4 47.4 all-gather.20
  263.3 47.4 all-gather.18
  470.8 73.5 reduce-scatter.14
  547.5 73.3 reduce-scatter.16
  624.1 73.2 reduce-scatter.22
  700.4 73.0 reduce-scatter.24
  776.6 73.2 reduce-scatter.18
  853.0 73.1 reduce-scatter.20
where the time goes:
time: 993 us; the launch traced here: 986 us
  matrix products  510 us (51%)
  waiting for transfers between devices  358 us (36%)
  blocking collectives  38.7 us (4%)
  local copies, waits for them, and re-layouts  30.8 us (3%)
  other arithmetic  29.3 us (3%)
  between operations  17.2 us (2%)
    unnamed x16, waiting for transfers between devices  253 us
    dot_general x5, matrix products, layer(): up = jnp.dot(a, w['w_up'], preferred_element_type=jnp.float32)  186 us
    dot_general x5, matrix products, layer(): gate = jnp.dot(a, w['w_gate'], preferred_element_type=jnp.float32)  179 us
    dot_general x5, matrix products, matmul(): jnp.dot(a, w, preferred_element_type=jnp.float32).astype(jnp.bfloat16)  145 us
    all_gather x6, waiting for transfers between devices, fetched(): lax.all_gather(w[number], 'dp', axis=0, tiled=True)  105 us
    psum x1, blocking collectives, step(): squares = lax.psum(sum((jnp.sum(g * g) for g in gradients)), 'dp')  38.7 us
    unnamed x30, local copies, waits for them, and re-layouts  25.1 us
  transfers between devices with their start and end apart: 12, of which 10 were waited for; matrix products, arithmetic and copies ran while one was open for 40% of the time, Pallas kernels for 0%

commit v1 on v0

v1 whole, which is shorter than its diff:
```python
import math

import jax
import jax.numpy as jnp
from jax import lax
from jax.experimental import pallas as pl
from jax.experimental.pallas import tpu as pltpu
from jax.sharding import PartitionSpec as P

MESH = pl.DeviceIdType.MESH
F32, BF16 = jnp.float32, jnp.bfloat16
ANY = pl.BlockSpec(memory_space=pl.ANY)
DMA = pltpu.SemaphoreType.DMA
CHUNK = 512
ROWS, TOKENS = 256, 512


class Spot:
    def __init__(self, side):
        self.side = side
        rep, self.dp = lax.axis_index("rep"), lax.axis_index("dp")
        c = self.c = lax.rem(rep, 2)
        hi, lo = self.dp // side, lax.rem(self.dp, side)
        self.f, self.s = hi * c + lo * (1 - c), lo * c + hi * (1 - c)
        self.partner = rep + 1 - 2 * c

    def at(self, f, s):
        f, s, c, side = lax.rem(f, self.side), lax.rem(s, self.side), self.c, self.side
        return f * (1 - c + side * c) + s * (side * (1 - c) + c)

    def near(self, df, ds):
        return self.at(self.f + df, self.s + ds)


def greet(places, partner=None):
    barrier = pltpu.get_barrier_semaphore()
    for place in places:
        pl.semaphore_signal(barrier, inc=1, device_id={"dp": place}, device_id_type=MESH)
    if partner is not None:
        pl.semaphore_signal(barrier, inc=1, device_id={"rep": partner}, device_id_type=MESH)
    pl.semaphore_wait(barrier, len(places) + (partner is not None))


def send(src, dst, out, came, **to):
    pltpu.make_async_remote_copy(src_ref=src, dst_ref=dst, send_sem=out, recv_sem=came, device_id=to, device_id_type=MESH).start()


def bring(src, dst, sem):
    pltpu.make_async_copy(src, dst, sem).start()


def await_bytes(like, sem):
    pltpu.make_async_copy(like, like, sem).wait()


def call(body, n, grid, in_specs, out_specs, out_shape, scratch, number, cost):
    def kernel(*refs):
        body(refs[:n], refs[n : n + len(out_shape)], refs[n + len(out_shape) :])

    return pl.pallas_call(
        kernel,
        grid=grid,
        in_specs=in_specs,
        out_specs=out_specs,
        out_shape=out_shape,
        scratch_shapes=scratch,
        compiler_params=pltpu.CompilerParams(
            dimension_semantics=("arbitrary",) * len(grid),
            vmem_limit_bytes=66_000_000,
            **({} if number is None else {"collective_id": number, "has_side_effects": True}),
        ),
        cost_estimate=pl.CostEstimate(flops=cost, bytes_accessed=cost // 400, transcendentals=0),
    )


def gather_scratch(rows, columns):
    return [pltpu.VMEM((rows, columns), BF16), DMA((2,)), DMA((2,)), DMA((6,))]


def gather_stages(spot, shards, layer, full, scratch):
    held, local, out, came = scratch
    rows, columns = held.shape
    by_columns = columns > 1024
    side = spot.side
    me, c = spot.dp, spot.c

    def part(ref, lead, cuts, number):
        if by_columns:
            width = columns // cuts
            return ref.at[lead, :, pl.ds(pl.multiple_of(number * width, 128), width)]
        height = rows // cuts
        return ref.at[lead, pl.ds(pl.multiple_of(number * height, 8), height), :]

    def unit(p):
        return part(full, p, 2, c)

    def quarter(p, q):
        return part(full, p, 4, 2 * c + q)

    def units(n):
        return part(full, pl.ds(0, n), 2, 0)

    def quarters(n):
        return part(full, pl.ds(0, n), 4, 0)

    mine = part(shards, layer, 2, c)

    def start():
        for df in (1, side - 1, 2):
            send(mine, unit(me), out.at[0], came.at[0], dp=spot.near(df, 0))
        fill = pltpu.make_async_copy(shards.at[layer], held, local.at[0])
        fill.start()
        fill.wait()
        bring(held, full.at[me], local.at[1])

    def across():
        await_bytes(units(side - 1), came.at[0])
        for df in range(side):
            p = spot.near(df, 0)
            source = unit(p) if df else mine
            send(source, unit(p), out.at[0], came.at[1], dp=spot.near(0, 1))
            send(source, unit(p), out.at[0], came.at[2], dp=spot.near(0, side - 1))
            if df:
                send(unit(p), unit(p), out.at[1], came.at[5], rep=spot.partner)

    def onward():
        await_bytes(units(side), came.at[1])
        await_bytes(units(side), came.at[2])
        for df in range(side):
            p, q = spot.near(df, side - 1), spot.near(df, 1)
            send(quarter(p, 0), quarter(p, 0), out.at[0], came.at[3], dp=spot.near(0, 1))
            send(quarter(q, 1), quarter(q, 1), out.at[0], came.at[4], dp=spot.near(0, side - 1))
        for df in range(side):
            for ds in (1, side - 1):
                p = spot.near(df, ds)
                send(unit(p), unit(p), out.at[1], came.at[5], rep=spot.partner)

    def last():
        await_bytes(quarters(side), came.at[3])
        await_bytes(quarters(side), came.at[4])
        for df in range(side):
            p = spot.near(df, 2)
            send(unit(p), unit(p), out.at[1], came.at[5], rep=spot.partner)

    def finish():
        n = side * side - 1
        await_bytes(units(n), came.at[5])
        await_bytes(units(n), out.at[0])
        await_bytes(units(n), out.at[1])
        await_bytes(held, local.at[1])

    return start, across, onward, last, finish


def greet_for_gather(spot):
    greet([spot.near(df, ds) for df, ds in ((1, 0), (spot.side - 1, 0), (2, 0), (0, 1), (0, spot.side - 1))], spot.partner)


def half_shape(rows, columns):
    return (rows, columns // 2) if columns > 1024 else (rows // 2, columns)


def half_of(ref, p, h):
    rows, columns = ref.shape[1:]
    if columns > 1024:
        return ref.at[p, :, pl.ds(h * (columns // 2), columns // 2)]
    return ref.at[p, pl.ds(h * (rows // 2), rows // 2), :]


def ring_scratch(n, half):
    return [pltpu.VMEM((n, *half), BF16)] * 10 + [DMA((4,)), DMA((6,)), DMA((6,))]


def ring_stages(source, place, side, plus, minus, scratch, own, done):
    across_a, across_b, next_a, prev_b, here_a, here_b, up_a, up_b, down_a, down_b, local, out, came = scratch
    n = across_a.shape[0]
    following, before, opposite = (lax.rem(place + d, side) for d in (1, side - 1, 2))

    def start():
        for k in range(n):
            send(source(opposite, k, 0), across_a.at[k], out.at[0], came.at[0], dp=plus)
            send(source(opposite, k, 1), across_b.at[k], out.at[1], came.at[1], dp=minus)
        for k in range(n):
            send(source(following, k, 1), up_b.at[k], out.at[2], came.at[2], dp=plus)
            send(source(before, k, 0), down_a.at[k], out.at[3], came.at[3], dp=minus)
        for k in range(n):
            bring(source(following, k, 0), next_a.at[k], local.at[0])
            bring(source(before, k, 1), prev_b.at[k], local.at[1])
            if own is None:
                bring(source(place, k, 0), here_a.at[k], local.at[2])
                bring(source(place, k, 1), here_b.at[k], local.at[3])

    def add():
        for which, (mine, theirs, landing, to) in enumerate(((next_a, across_a, up_a, plus), (prev_b, across_b, down_b, minus))):
            await_bytes(mine, local.at[which])
            await_bytes(theirs, came.at[which])
            for k in range(n):
                mine[k] = (mine[k].astype(F32) + theirs[k].astype(F32)).astype(BF16)
            for k in range(n):
                send(mine.at[k], landing.at[k], out.at[4 + which], came.at[4 + which], dp=to)

    def finish():
        if own is None:
            await_bytes(here_a, local.at[2])
            await_bytes(here_b, local.at[3])
        for number, ref in zip((2, 3, 4, 5), (up_b, down_a, up_a, down_b), strict=True):
            await_bytes(ref, came.at[number])
        for k in range(n):
            for h, here, up, down in ((0, here_a, up_a, down_a), (1, here_b, up_b, down_b)):
                term = here[k].astype(F32) if own is None else own[h]
                done(k, h, term + up[k].astype(F32) + down[k].astype(F32))
        for number in range(6):
            await_bytes(across_a, out.at[number])

    return start, add, finish


def first_ring(spot, blocks, scratch, partial, kept):
    def done(k, h, total):
        partial[k, h] = total.astype(BF16)

        @pl.when(spot.s == k)
        def _():
            kept[h] = total

    def source(j, k, h):
        return half_of(blocks, spot.at(j, k), h)

    return ring_stages(source, spot.f, spot.side, spot.near(1, 0), spot.near(spot.side - 1, 0), scratch, None, done)


def second_ring(spot, partial, kept, scratch, result):
    def done(k, h, total):
        result[h] = total.astype(BF16)

    def source(j, k, h):
        return partial.at[j, h]

    return ring_stages(source, spot.s, spot.side, spot.near(0, 1), spot.near(0, spot.side - 1), scratch, kept, done)


def dot(a, b):
    return jnp.dot(a, b, preferred_element_type=F32)


def dot_t(a, b):
    return lax.dot_general(a, b, (((1,), (1,)), ((), ())), preferred_element_type=F32)


def scale_of(wide):
    return lax.rsqrt(jnp.mean(wide * wide, -1, keepdims=True) + 1e-6)


def gated_back(gate, up, by_act):
    s = jax.nn.sigmoid(gate)
    silu = gate * s
    return silu, (by_act * up * (s + silu * (1 - s))).astype(BF16), (by_act * silu).astype(BF16)


def cuts(n):
    return [pl.ds(at, CHUNK) for at in range(0, n, CHUNK)]


def put_blocks(out, total):
    blocks, rows, _ = out.shape
    for p in range(blocks):
        out[p] = total[pl.ds(p * rows, rows), :].astype(BF16)


def whole(shape):
    return pl.BlockSpec(shape, lambda i: (0,) * len(shape), pipeline_mode=pl.Buffered(1))


def fixed(shape):
    return pl.BlockSpec(shape, lambda i: (0,) * len(shape))


def tile(rows, columns):
    return pl.BlockSpec((rows, columns), lambda i: (i, 0))


def tile_of_one(rows, columns):
    return pl.BlockSpec((None, rows, columns), lambda i: (0, i, 0))


def struct(shape, dtype=BF16):
    return jax.ShapeDtypeStruct(shape, dtype)


def solution(mesh):
    group = mesh.shape["dp"]
    side = math.isqrt(group)

    def gather_only(shards, layer):
        shapes = [w.shape[1:] for w in shards]

        def body(ins, outs, scratch):
            spot = Spot(side)
            greet_for_gather(spot)
            stages = [gather_stages(spot, ins[i], layer, outs[i], scratch[4 * i : 4 * i + 4]) for i in range(3)]
            for stage in zip(*stages, strict=True):
                for run in stage:
                    run()

        scratch = [one for shape in shapes for one in gather_scratch(*shape)]
        outs = [struct((group, *shape)) for shape in shapes]
        return call(body, 3, (), [ANY] * 3, [ANY] * 3, outs, scratch, 0, 1000)(*shards)

    def forward(x, weights, shards, layer):
        _, tokens, d = x.shape
        ff = weights[0].shape[1]
        steps = tokens // ROWS
        shapes = [w.shape[1:] for w in shards]

        def body(ins, outs, scratch):
            x, w_gate, w_up, w_down, *shards = ins
            a_out, gate_out, up_out, act_out, h_out, *full = outs
            i = pl.program_id(0)
            spot = Spot(side)
            stages = [gather_stages(spot, shards[j], layer, full[j], scratch[4 * j : 4 * j + 4]) for j in range(3)]
            for number, when in enumerate((0, 3, 8, 11)):

                @pl.when(i == when)
                def _():
                    if number == 0:
                        greet_for_gather(spot)
                    for one in stages:
                        one[number]()

            wide = x[...].astype(F32)
            a = (wide * scale_of(wide)).astype(BF16)
            a_out[...] = a
            for cut in cuts(ff):
                gate, up = dot(a, w_gate[:, cut]), dot(a, w_up[:, cut])
                gate_out[:, cut], up_out[:, cut] = gate, up
                act_out[:, cut] = (gate * jax.nn.sigmoid(gate) * up).astype(BF16)
            h_out[...] = (wide + dot(act_out[...], w_down[...]).astype(BF16).astype(F32)).astype(BF16)

            @pl.when(i == steps - 1)
            def _():
                for one in stages:
                    one[4]()

        scratch = [one for shape in shapes for one in gather_scratch(*shape)]
        wide = [struct((tokens, ff), F32)] * 2
        outs = [struct((tokens, d)), *wide, struct((tokens, ff)), struct((tokens, d))] + [struct((group, *s)) for s in shapes]
        out_specs = [tile(ROWS, d)] + [tile(ROWS, ff)] * 3 + [tile(ROWS, d)] + [ANY] * 3
        in_specs = [tile_of_one(ROWS, d)] + [whole(w.shape) for w in weights] + [ANY] * 3
        return call(body, 7, (steps,), in_specs, out_specs, outs, scratch, 1, 6 * tokens * d * ff)(x, *weights, *shards)

    def last_layer(h, dy, weights):
        tokens, d = h.shape
        ff = weights[0].shape[1]
        steps = tokens // ROWS
        rows = ff // group

        def body(ins, outs, scratch):
            h, dy, w_gate, w_up, w_down = ins
            a_out, by_gate, by_up, by_h, by_down = outs
            total, act = scratch
            i = pl.program_id(0)

            @pl.when(i == 0)
            def _():
                total[...] = jnp.zeros_like(total)

            wide = h[...].astype(F32)
            scale = scale_of(wide)
            a = (wide * scale).astype(BF16)
            a_out[...] = a
            by_y = dy[...]
            for cut in cuts(ff):
                gate, up = dot(a, w_gate[:, cut]), dot(a, w_up[:, cut])
                by_act = dot_t(by_y, w_down[cut, :]).astype(BF16).astype(F32)
                silu, by_gate[:, cut], by_up[:, cut] = gated_back(gate, up, by_act)
                act[:, cut] = (silu * up).astype(BF16)
            by_a = dot_t(by_gate[...], w_gate[...]).astype(BF16).astype(F32) + dot_t(by_up[...], w_up[...]).astype(BF16).astype(F32)
            by_a = by_a.astype(BF16).astype(F32)
            inner = jnp.sum(by_a * wide, -1, keepdims=True) * (scale * scale * scale) * (1 / d)
            by_x = (by_a * scale - wide * inner).astype(BF16)
            by_h[...] = (by_y.astype(F32) + by_x.astype(F32)).astype(BF16)
            for cut in cuts(ff):
                total[cut, :] += dot(act[:, cut].T, by_y)

            @pl.when(i == steps - 1)
            def _():
                put_blocks(by_down, total)

        outs = [struct((tokens, d)), struct((tokens, ff)), struct((tokens, ff)), struct((tokens, d)), struct((group, rows, d))]
        out_specs = [tile(ROWS, d), tile(ROWS, ff), tile(ROWS, ff), tile(ROWS, d), fixed((group, rows, d))]
        in_specs = [tile(ROWS, d), tile_of_one(ROWS, d)] + [whole(w.shape) for w in weights]
        scratch = [pltpu.VMEM((ff, d), F32), pltpu.VMEM((ROWS, ff), BF16)]
        return call(body, 5, (steps,), in_specs, out_specs, outs, scratch, None, 12 * tokens * d * ff)(h, dy, *weights)

    def hidden(compute, n_in, n_out, steps, number, first, second):
        more_in, more_specs, more_out, more_out_specs, more_scratch = [], [], [], [], []
        if first is not None:
            half = half_shape(*first.shape[1:])
            more_in += [first]
            more_specs += [ANY]
            more_out += [struct((side, 2, *half)), struct((2, *half), F32)]
            more_out_specs += [fixed((side, 2, *half)), fixed((2, *half))]
            more_scratch += ring_scratch(side, half)
        if second is not None:
            partial, kept = second
            half = partial.shape[2:]
            more_in += [partial, kept]
            more_specs += [ANY, whole(kept.shape)]
            more_out += [struct((2, *half))]
            more_out_specs += [fixed((2, *half))]
            more_scratch += ring_scratch(1, half)

        def body(ins, outs, scratch):
            i = pl.program_id(0)
            spot = Spot(side)
            own = len(scratch) - len(more_scratch)
            ins_left, outs_left, scratch_left = list(ins[n_in:]), list(outs[n_out:]), list(scratch[own:])
            plan = []
            if first is not None:
                stages = first_ring(spot, ins_left.pop(0), scratch_left[:13], outs_left.pop(0), outs_left.pop(0))
                del scratch_left[:13]
                plan += list(zip((0, (5 * steps) // 8, None), stages, strict=True))
            if second is not None:
                stages = second_ring(spot, ins_left.pop(0), ins_left.pop(0), scratch_left, outs_left.pop(0))
                plan += list(zip((0, (3 * steps) // 8, (6 * steps) // 8), stages, strict=True))

            @pl.when(i == 0)
            def _():
                greet([spot.near(*way) for way in ((1, 0), (side - 1, 0), (0, 1), (0, side - 1))])

            for when, run in plan:
                if when is not None:
                    pl.when(i == when)(run)
            compute(i, ins[:n_in], outs[:n_out], scratch[:own])
            for when, run in plan:
                if when is None:
                    pl.when(i == steps - 1)(run)

        return body, more_in, more_specs, more_out, more_out_specs, more_scratch

    def weight_gradient(a, by, number, first, second):
        tokens, m = a.shape
        n = by.shape[1]
        steps = tokens // TOKENS
        rows = m // group

        def compute(i, ins, outs, scratch):
            a, by = ins
            (total,) = scratch

            @pl.when(i == 0)
            def _():
                total[...] = jnp.zeros_like(total)

            if n > m:
                left = a[...].T
                for cut in cuts(n):
                    total[:, cut] += dot(left, by[:, cut])
            else:
                right = by[...]
                for cut in cuts(m):
                    total[cut, :] += dot(a[:, cut].T, right)

            @pl.when(i == steps - 1)
            def _():
                put_blocks(outs[0], total)

        body, ins, specs, outs, out_specs, scratch = hidden(compute, 2, 1, steps, number, first, second)
        return call(
            body,
            2 + len(ins),
            (steps,),
            [tile(TOKENS, m), tile(TOKENS, n), *specs],
            [fixed((group, rows, n)), *out_specs],
            [struct((group, rows, n)), *outs],
            [pltpu.VMEM((m, n), F32), *scratch],
            number,
            2 * tokens * m * n,
        )(a, by, *ins)

    def gate_gradient(by_h, gate, up, a, w_down, number, first, second):
        tokens, d = a.shape
        ff = gate.shape[1]
        steps = tokens // ROWS
        rows = d // group

        def compute(i, ins, outs, scratch):
            by_h, gate, up, a, w_down = ins
            by_up, by_w = outs
            (total,) = scratch

            @pl.when(i == 0)
            def _():
                total[...] = jnp.zeros_like(total)

            by_y, left = by_h[...], a[...].T
            for cut in cuts(ff):
                by_act = dot_t(by_y, w_down[cut, :]).astype(BF16).astype(F32)
                _, by_gate, by_up[:, cut] = gated_back(gate[:, cut], up[:, cut], by_act)
                total[:, cut] += dot(left, by_gate)

            @pl.when(i == steps - 1)
            def _():
                put_blocks(by_w, total)

        body, ins, specs, outs, out_specs, scratch = hidden(compute, 5, 2, steps, number, first, second)
        return call(
            body,
            5 + len(ins),
            (steps,),
            [tile(ROWS, d), tile(ROWS, ff), tile(ROWS, ff), tile(ROWS, d), whole(w_down.shape), *specs],
            [tile(ROWS, ff), fixed((group, rows, ff)), *out_specs],
            [struct((tokens, ff)), struct((group, rows, ff)), *outs],
            [pltpu.VMEM((d, ff), F32), *scratch],
            number,
            4 * tokens * d * ff,
        )(by_h, gate, up, a, w_down, *ins)

    def closing(first, second, ready, number):
        half = half_shape(*first.shape[1:])
        n = len(ready)

        def body(ins, outs, scratch):
            blocks, partial, kept, *ready = ins
            late, last, squares = outs
            spot = Spot(side)
            greet([spot.near(*way) for way in ((1, 0), (side - 1, 0), (2, 0), (0, 1), (0, side - 1), (0, 2))])
            ring_1, ring_2, ring_3 = scratch[:13], scratch[13:26], scratch[26:39]
            partial_2, kept_2, sums, out, came = scratch[39:]
            one = first_ring(spot, blocks, ring_1, partial_2, kept_2)
            two = second_ring(spot, partial, kept, ring_2, late)
            three = second_ring(spot, partial_2, kept_2, ring_3, last)
            one[0]()
            two[0]()
            two[1]()
            one[1]()
            two[2]()
            total = jnp.zeros((1, 1), F32)
            for g in [*ready, late]:
                for h in range(2):
                    wide = g[h].astype(F32)
                    total += jnp.sum(wide * wide, keepdims=True)
            one[2]()
            three[0]()
            three[1]()
            three[2]()
            for h in range(2):
                wide = last[h].astype(F32)
                total += jnp.sum(wide * wide, keepdims=True)
            for axis in range(2):
                sums[axis, 0] = jnp.broadcast_to(total, sums.shape[2:])
                for d in range(1, side):
                    to = spot.near(d, 0) if axis == 0 else spot.near(0, d)
                    send(sums.at[axis, 0], sums.at[axis, d], out.at[axis, d - 1], came.at[axis, d - 1], dp=to)
                for d in range(1, side):
                    await_bytes(sums.at[axis, 0], came.at[axis, d - 1])
                for d in range(1, side):
                    total = total + sums[axis, d, 0:1, 0:1]
                for d in range(1, side):
                    await_bytes(sums.at[axis, 0], out.at[axis, d - 1])
            squares[...] = jnp.broadcast_to(total, squares.shape)

        vmem = pl.BlockSpec(memory_space=pltpu.VMEM)
        partial, kept = second
        scratch = ring_scratch(side, half) + ring_scratch(1, half) * 2
        scratch += [pltpu.VMEM((side, 2, *half), BF16), pltpu.VMEM((2, *half), F32), pltpu.VMEM((2, side, 8, 128), F32)]
        scratch += [DMA((2, side - 1)), DMA((2, side - 1))]
        outs = [struct((2, *half)), struct((2, *half)), struct((8, 128), F32)]
        return call(body, 3 + n, (), [ANY, ANY, vmem] + [vmem] * n, [vmem] * 3, outs, scratch, number, 1000)(first, partial, kept, *ready)

    def adamw(w, m, v, g):
        m = 0.9 * m + 0.1 * g
        v = 0.95 * v + 0.05 * g * g
        step = m * lax.rsqrt(v + 1e-8) + 0.1 * w
        return (w - 0.02 * step).astype(BF16), m, v

    def joined(g, shape):
        return jnp.concatenate([g[0], g[1]], 1 if shape[1] > 1024 else 0)

    def step(x, dy, *arrays):
        weights, m, v = (arrays[i : i + 3] for i in (0, 3, 6))
        flat = lambda full: [w.reshape(-1, w.shape[2]) for w in full]
        w_0 = flat(gather_only(weights, 0))
        a_0, gate, up, act, h, *full = forward(x, w_0, weights, 1)
        a_1, by_gate, by_up, by_h, down_1 = last_layer(h, dy, flat(full))
        gate_1, *down_1 = weight_gradient(a_1, by_gate, 2, down_1, None)
        up_1, *gate_1, down_1 = weight_gradient(a_1, by_up, 3, gate_1, down_1)
        down_0, *up_1, gate_1 = weight_gradient(act, by_h, 4, up_1, gate_1)
        by_up, gate_0, *down_0, up_1 = gate_gradient(by_h, gate, up, a_0, w_0[2], 5, down_0, up_1)
        up_0, *gate_0, down_0 = weight_gradient(a_0, by_up, 6, gate_0, down_0)
        gate_0, up_0, squares = closing(up_0, gate_0, [down_1, gate_1, up_1, down_0], 7)
        count = group * sum(w.size for w in weights)
        factor = jnp.minimum(1.0, 0.5 * lax.rsqrt(squares[0, 0] / count + 1e-30))
        pairs = ((gate_0, gate_1), (up_0, up_1), (down_0, down_1))
        new = []
        for w, m_w, v_w, pair in zip(weights, m, v, pairs, strict=True):
            g = jnp.stack([joined(one, w.shape[1:]) for one in pair]).astype(F32) * factor
            new.append(adamw(w.astype(F32), m_w, v_w, g))
        return tuple(one[which] for which in range(3) for one in new)

    states, cut = P(("rep", "dp"), None, None), P(None, "dp", None)
    return jax.shard_map(
        step,
        mesh=mesh,
        in_specs=(states, states) + (cut,) * 9,
        out_specs=(P("rep", "dp", None),) * 9,
        check_vma=False,
    )
```

time: 993 us -> 564 us (0.57)
  Pallas kernels: 0 us -> 543 us
  matrix products: 510 us -> 0 us
  waiting for transfers between devices: 358 us -> 0 us
  blocking collectives: 38.7 us -> 0 us
  local copies, waits for them, and re-layouts: 30.8 us -> 6.8 us
  other arithmetic: 29.3 us -> 5.86 us
  between operations: 17.2 us -> 1.97 us
    pallas_call x0 -> x9, Pallas kernels: none -> 543 us  [the longest x1 157 us: last_layer(): call(body, 5, (steps,), in_specs, out_specs, outs, scratch, None, 12 * to...]
    dot_general x15 -> x0, matrix products: 510 us -> none  [the longest x5 186 us: layer(): up = jnp.dot(a, w['w_up'], preferred_element_type=jnp.float32)]
    unnamed x16 -> x0, waiting for transfers between devices: 253 us -> none
    all_gather x6 -> x0, waiting for transfers between devices: 105 us -> none  [fetched(): lax.all_gather(w[number], 'dp', axis=0, tiled=True)]
    psum x1 -> x0, blocking collectives: 38.7 us -> none  [step(): squares = lax.psum(sum((jnp.sum(g * g) for g in gradients)), 'dp')]
    unnamed x30 -> x26, local copies, waits for them, and re-layouts: 25.1 us -> 4.28 us
    reduce_sum x4 -> x0, other arithmetic: 10.5 us -> none  [the longest x3 5.95 us: step(): squares = lax.psum(sum((jnp.sum(g * g) for g in gradients)), 'dp')]
  transfers between devices with their start and end apart: 12 -> 0, of which waited for: 10 -> 0; matrix products, arithmetic and copies ran while one was open for 40% -> 0% of each run, Pallas kernels for 0% -> 0%
where the time goes in v1:
time: 564 us; the launch traced here: 557 us
  Pallas kernels  543 us (96%)
  local copies, waits for them, and re-layouts  6.8 us (1%)
  other arithmetic  5.86 us (1%)
    pallas_call x1, Pallas kernels, last_layer(): call(body, 5, (steps,), in_specs, out_specs, outs, scratch, None, 12 * to...  157 us
    pallas_call x4, Pallas kernels, weight_gradient(): call(body, 2 + len(ins), (steps,), [tile(TOKENS, m), tile(TOKENS, n), *sp...  128 us
    pallas_call x1, Pallas kernels, forward(): call(body, 7, (steps,), in_specs, out_specs, outs, scratch, 1, 6 * tokens...  87.2 us
    pallas_call x1, Pallas kernels, gate_gradient(): call(body, 5 + len(ins), (steps,), [tile(ROWS, d), tile(ROWS, ff), tile(R...  76.3 us
    pallas_call x1, Pallas kernels, gather_only(): call(body, 3, (), [ANY] * 3, [ANY] * 3, outs, scratch, 0, 1000)(*shards)  47.3 us
    pallas_call x1, Pallas kernels, closing(): call(body, 3 + n, (), [ANY, ANY, vmem] + [vmem] * n, [vmem] * 3, outs, sc...  46.6 us

profile of v1, /device:TPU:96, one launch (start us, length us, event | category | flops | bytes accessed | tf_op | source)
XLA Modules:
  0.0 557.2 jit_solution(4946060435505823634)
XLA Ops:
  0.6 47.3 %shard_map.178 = (bf16[16,56,2560]{2,1,0:T(8,128)(2,1)}, bf16[16,56,2560]{2,1,0:T(8,128)(2,1)}, bf16[16,160,896]{2,1,0:T(8,128)(2,1)}) custom-call(bf16[2,56,2560]{2,1,0:T(8,128)(2,1)} %refs_4_.1, bf16[2,56,2560]{2,1,0:T(8,128)(2,1)} %refs_5_.1, bf16[2,160,896]{2,1,0:T(8,128)(2,1)} %refs_6_.1), custom_call_target="tpu_custom_call" | custom-call | flops 1000 | bytes 2 | tf_op jit(solution)/shard_map/pallas_call | solution.py:307
  47.9 87.2 %shard_map.179 = (bf16[4096,896]{1,0:T(8,128)(2,1)}, f32[4096,2560]{1,0:T(8,128)}, f32[4096,2560]{1,0:T(8,128)}, bf16[4096,2560]{1,0:T(8,128)(2,1)}, bf16[4096,8...) custom-call(bf16[1,4096,896]{2,1,0:T(8,128)(2,1)} %refs_0_.3, ...), custom_call_target="tpu_custom_call" | custom-call | flops 56371445760 | bytes 140928608 | tf_op jit(solution)/shard_map/pallas_call | solution.py:349
  135.1 157.2 %shard_map.180 = (bf16[4096,896]{1,0:T(8,128)(2,1)}, bf16[4096,2560]{1,0:T(8,128)(2,1)}, bf16[4096,2560]{1,0:T(8,128)(2,1)}, bf16[4096,896]{1,0:T(8,128)(2,1)}, bf16[16,160,896]{2,1,0:T(8,128)(2,1)}) custom-call(bf16[4096,896]{1,0:T(8,128)(2,1)} %get-tuple-element.52.refs_0_, bf16[1,4096,896]{2,1,0:T(8,128)(2,1)} %refs_1_.3, bf16[896,2560]{1,0:T(8,128)(2,1)} %bitcast.47, ...), custom_call_target="tpu_custom_call" | custom-call | flops 112742891520 | bytes 281857216 | tf_op jit(solution)/shard_map/pallas_call | solution.py:393
  292.3 30.3 %shard_map.181 = (bf16[16,56,2560]{2,1,0:T(8,128)(2,1)}, bf16[4,2,80,896]{3,2,1,0:T(8,128)(2,1)}, f32[2,80,896]{2,1,0:T(8,128)}) custom-call(bf16[4096,896]{1,0:T(8,128)(2,1)} %get-tuple-element.60.refs_0_, bf16[4096,2560]{1,0:T(8,128)(2,1)} %get-tuple-element.62.refs_1_, bf16[16,160,896]{2,1,0:T(8,128)(2,1)} %get-tuple-element.63.refs_2_), custom_call_target="tpu_custom_call" | custom-call | flops 18790481920 | bytes 46976204 | tf_op jit(solution)/shard_map/pallas_call | solution.py:469
  322.6 31.7 %shard_map.182 = (bf16[16,56,2560]{2,1,0:T(8,128)(2,1)}, bf16[4,2,56,1280]{3,2,1,0:T(8,128)(2,1)}, f32[2,56,1280]{2,1,0:T(8,128)}, bf16[2,80,896]{2,1,0:T(8,128)(2,1)}) custom-call(bf16[4096,896]{1,0:T(8,128)(2,1)} %get-tuple-element.60.refs_0_, bf16[4096,2560]{1,0:T(8,128)(2,1)} %get-tuple-element.61.refs_1_, ...), custom_call_target="tpu_custom_call" | custom-call | flops 18790481920 | bytes 46976204 | tf_op jit(solution)/shard_map/pallas_call | solution.py:469
  354.3 33.8 %shard_map.183 = (bf16[16,160,896]{2,1,0:T(8,128)(2,1)}, bf16[4,2,56,1280]{3,2,1,0:T(8,128)(2,1)}, f32[2,56,1280]{2,1,0:T(8,128)}, bf16[2,56,1280]{2,1,0:T(8,128)(2,1)}) custom-call(bf16[4096,2560]{1,0:T(8,128)(2,1)} %get-tuple-element.59.refs_0_, bf16[4096,896]{1,0:T(8,128)(2,1)} %get-tuple-element.56.refs_1_.refs_0_, ...), custom_call_target="tpu_custom_call" | custom-call | flops 18790481920 | bytes 46976204 | tf_op jit(solution)/shard_map/pallas_call | solution.py:469
  388.1 76.3 %shard_map.184 = (bf16[4096,2560]{1,0:T(8,128)(2,1)}, bf16[16,56,2560]{2,1,0:T(8,128)(2,1)}, bf16[4,2,80,896]{3,2,1,0:T(8,128)(2,1)}, f32[2,80,896]{2,1,0:T(8,128)}, bf16[2,56,1280]{2,1,0:T(8,128)(2,1)}) custom-call(bf16[4096,896]{1,0:T(8,128)(2,1)} %get-tuple-element.56.refs_1_.refs_0_, f32[4096,2560]{1,0:T(8,128)} %get-tuple-element.57.refs_1_, ...), custom_call_target="tpu_custom_call" | custom-call | flops 37580963840 | bytes 93952408 | tf_op jit(solution)/shard_map/pallas_call | solution.py:507
  464.4 32.3 %shard_map.185 = (bf16[16,56,2560]{2,1,0:T(8,128)(2,1)}, bf16[4,2,56,1280]{3,2,1,0:T(8,128)(2,1)}, f32[2,56,1280]{2,1,0:T(8,128)}, bf16[2,80,896]{2,1,0:T(8,128)(2,1)}) custom-call(bf16[4096,896]{1,0:T(8,128)(2,1)} %get-tuple-element.51.refs_3_.refs_0_, bf16[4096,2560]{1,0:T(8,128)(2,1)} %get-tuple-element.73.refs_1_, ...), custom_call_target="tpu_custom_call" | custom-call | flops 18790481920 | bytes 46976204 | tf_op jit(solution)/shard_map/pallas_call | solution.py:469
  496.7 46.6 %shard_map.186 = (bf16[2,56,1280]{2,1,0:T(8,128)(2,1)}, bf16[2,56,1280]{2,1,0:T(8,128)(2,1)}, f32[8,128]{1,0:T(8,128)}) custom-call(bf16[16,56,2560]{2,1,0:T(8,128)(2,1)} %get-tuple-element.77.refs_0_, bf16[4,2,56,1280]{3,2,1,0:T(8,128)(2,1)} %get-tuple-element.78.refs_1_, f32[2,56,1280]{2,1,0:T(8,128)} %get-tuple-element.79.refs_2_, ...), custom_call_target="tpu_custom_call" | custom-call | flops 1000 | bytes 2 | tf_op jit(solution)/shard_map/pallas_call | solution.py:569
  543.3 0.0 copy-start.12
  543.3 1.2 slice.43
  545.2 0.0 copy-start.11
  545.3 1.2 slice_bitcast_fusion.7
  546.5 0.0 copy-start.10
  546.5 0.0 copy-done.12
  546.5 0.0 copy-done.11
  546.5 0.0 copy-start.9
  546.6 0.8 copy-done.10
  547.4 0.0 copy-start.4
  547.5 0.0 copy-done.9
  547.5 0.0 copy-start
  547.5 0.0 copy-start.3
  547.6 0.1 maximum_bitcast_fusion.4
  547.6 1.1 copy-done.4
  548.7 0.1 copy-done
  548.9 0.4 copy-done.3
  549.2 0.0 copy-start.1
  549.2 0.0 copy-start.5
  549.2 0.0 copy-start.6
  549.2 1.9 fusion.2
  551.2 0.0 copy-done.1
  551.2 0.1 copy-done.5
  551.2 0.8 copy-done.6
  552.1 0.0 copy-start.2
  552.1 0.0 copy-start.7
  552.1 0.0 copy-start.8
  552.1 1.9 fusion.8
  554.0 0.0 copy-done.2
  554.0 0.2 copy-done.7
  554.1 0.7 copy-done.8
  554.9 1.9 fusion.5
  (8 shorter events, 0.2 us)
Async XLA Ops:
  543.3 3.2 copy-start.12
  545.2 1.3 copy-start.11
  546.5 1.0 copy-start.10
  546.5 1.0 copy-start.9
  547.4 1.3 copy-start.4
  547.5 1.3 copy-start
  547.5 1.7 copy-start.3
  549.2 1.9 copy-start.1
  549.2 2.0 copy-start.5
  549.2 2.8 copy-start.6
  552.1 1.9 copy-start.2
  552.1 2.1 copy-start.7
  552.1 2.8 copy-start.8

commit v2 on v1

--- a/solution.py
+++ b/solution.py
@@ -74,7 +74,7 @@
 
 
 def gather_scratch(rows, columns):
-    return [pltpu.VMEM((rows, columns), BF16), DMA((2,)), DMA((2,)), DMA((6,))]
+    return [pltpu.VMEM((rows, columns), BF16), DMA((2,)), DMA((2,)), DMA((9,))]
 
 
 def gather_stages(spot, shards, layer, full, scratch):
@@ -106,15 +106,23 @@
     mine = part(shards, layer, 2, c)
 
     def start():
-        for df in (1, side - 1, 2):
-            send(mine, unit(me), out.at[0], came.at[0], dp=spot.near(df, 0))
+        send(mine, unit(me), out.at[0], came.at[0], dp=spot.near(1, 0))
+        send(mine, unit(me), out.at[0], came.at[6], dp=spot.near(side - 1, 0))
         fill = pltpu.make_async_copy(shards.at[layer], held, local.at[0])
         fill.start()
         fill.wait()
         bring(held, full.at[me], local.at[1])
 
+    def relay():
+        p, q = spot.near(side - 1, 0), spot.near(1, 0)
+        await_bytes(unit(p), came.at[0])
+        send(quarter(p, 0), quarter(p, 0), out.at[0], came.at[7], dp=spot.near(1, 0))
+        await_bytes(unit(q), came.at[6])
+        send(quarter(q, 1), quarter(q, 1), out.at[0], came.at[8], dp=spot.near(side - 1, 0))
+
     def across():
-        await_bytes(units(side - 1), came.at[0])
+        await_bytes(quarter(me, 0), came.at[7])
+        await_bytes(quarter(me, 1), came.at[8])
         for df in range(side):
             p = spot.near(df, 0)
             source = unit(p) if df else mine
@@ -149,11 +157,11 @@
         await_bytes(units(n), out.at[1])
         await_bytes(held, local.at[1])
 
-    return start, across, onward, last, finish
+    return start, relay, across, onward, last, finish
 
 
 def greet_for_gather(spot):
-    greet([spot.near(df, ds) for df, ds in ((1, 0), (spot.side - 1, 0), (2, 0), (0, 1), (0, spot.side - 1))], spot.partner)
+    greet([spot.near(df, ds) for df, ds in ((1, 0), (spot.side - 1, 0), (0, 1), (0, spot.side - 1))], spot.partner)
 
 
 def half_shape(rows, columns):
@@ -318,7 +326,7 @@
             i = pl.program_id(0)
             spot = Spot(side)
             stages = [gather_stages(spot, shards[j], layer, full[j], scratch[4 * j : 4 * j + 4]) for j in range(3)]
-            for number, when in enumerate((0, 3, 8, 11)):
+            for number, when in enumerate((0, 2, 4, 9, 12)):
 
                 @pl.when(i == when)
                 def _():
@@ -339,7 +347,7 @@
             @pl.when(i == steps - 1)
             def _():
                 for one in stages:
-                    one[4]()
+                    one[5]()
 
         scratch = [one for shape in shapes for one in gather_scratch(*shape)]
         wide = [struct((tokens, ff), F32)] * 2
@@ -392,17 +400,17 @@
         scratch = [pltpu.VMEM((ff, d), F32), pltpu.VMEM((ROWS, ff), BF16)]
         return call(body, 5, (steps,), in_specs, out_specs, outs, scratch, None, 12 * tokens * d * ff)(h, dy, *weights)
 
-    def hidden(compute, n_in, n_out, steps, number, first, second):
+    def hidden(compute, n_in, n_out, n_scratch, firsts, seconds):
         more_in, more_specs, more_out, more_out_specs, more_scratch = [], [], [], [], []
-        if first is not None:
-            half = half_shape(*first.shape[1:])
-            more_in += [first]
-            more_specs += [ANY]
+        for _, blocks, shape in firsts:
+            half = half_shape(*shape)
+            if not isinstance(blocks, int):
+                more_in += [blocks]
+                more_specs += [ANY]
             more_out += [struct((side, 2, *half)), struct((2, *half), F32)]
             more_out_specs += [fixed((side, 2, *half)), fixed((2, *half))]
             more_scratch += ring_scratch(side, half)
-        if second is not None:
-            partial, kept = second
+        for _, (partial, kept) in seconds:
             half = partial.shape[2:]
             more_in += [partial, kept]
             more_specs += [ANY, whole(kept.shape)]
@@ -413,32 +421,33 @@
         def body(ins, outs, scratch):
             i = pl.program_id(0)
             spot = Spot(side)
-            own = len(scratch) - len(more_scratch)
-            ins_left, outs_left, scratch_left = list(ins[n_in:]), list(outs[n_out:]), list(scratch[own:])
+            ins_left, outs_left, rings = list(ins[n_in:]), list(outs[n_out:]), list(scratch[n_scratch:])
             plan = []
-            if first is not None:
-                stages = first_ring(spot, ins_left.pop(0), scratch_left[:13], outs_left.pop(0), outs_left.pop(0))
-                del scratch_left[:13]
-                plan += list(zip((0, (5 * steps) // 8, None), stages, strict=True))
-            if second is not None:
-                stages = second_ring(spot, ins_left.pop(0), ins_left.pop(0), scratch_left, outs_left.pop(0))
-                plan += list(zip((0, (3 * steps) // 8, (6 * steps) // 8), stages, strict=True))
+            for when, blocks, _ in firsts:
+                source = scratch[blocks] if isinstance(blocks, int) else ins_left.pop(0)
+                stages = first_ring(spot, source, rings[:13], outs_left.pop(0), outs_left.pop(0))
+                del rings[:13]
+                plan += list(zip(when, stages, strict=True))
+            for when, _ in seconds:
+                stages = second_ring(spot, ins_left.pop(0), ins_left.pop(0), rings[:13], outs_left.pop(0))
+                del rings[:13]
+                plan += list(zip(when, stages, strict=True))
 
             @pl.when(i == 0)
             def _():
                 greet([spot.near(*way) for way in ((1, 0), (side - 1, 0), (0, 1), (0, side - 1))])
 
             for when, run in plan:
-                if when is not None:
+                if when >= 0:
                     pl.when(i == when)(run)
-            compute(i, ins[:n_in], outs[:n_out], scratch[:own])
+            compute(i, ins[:n_in], outs[:n_out], scratch[:n_scratch])
             for when, run in plan:
-                if when is None:
-                    pl.when(i == steps - 1)(run)
+                if when < 0:
+                    pl.when(i == pl.num_programs(0) + when)(run)
 
         return body, more_in, more_specs, more_out, more_out_specs, more_scratch
 
-    def weight_gradient(a, by, number, first, second):
+    def weight_gradient(a, by, number, firsts, seconds):
         tokens, m = a.shape
         n = by.shape[1]
         steps = tokens // TOKENS
@@ -452,20 +461,15 @@
             def _():
                 total[...] = jnp.zeros_like(total)
 
-            if n > m:
-                left = a[...].T
-                for cut in cuts(n):
-                    total[:, cut] += dot(left, by[:, cut])
-            else:
-                right = by[...]
-                for cut in cuts(m):
-                    total[cut, :] += dot(a[:, cut].T, right)
+            right = by[...]
+            for cut in cuts(m):
+                total[cut, :] += dot(a[:, cut].T, right)
 
             @pl.when(i == steps - 1)
             def _():
                 put_blocks(outs[0], total)
 
-        body, ins, specs, outs, out_specs, scratch = hidden(compute, 2, 1, steps, number, first, second)
+        body, ins, specs, outs, out_specs, scratch = hidden(compute, 2, 1, 1, firsts, seconds)
         return call(
             body,
             2 + len(ins),
@@ -478,10 +482,58 @@
             2 * tokens * m * n,
         )(a, by, *ins)
 
-    def gate_gradient(by_h, gate, up, a, w_down, number, first, second):
+    def two_gradients(a, bys, width, number, firsts, seconds):
+        tokens, m = a.shape
+        steps = tokens // TOKENS
+        rows = m // group
+
+        def compute(i, ins, outs, scratch):
+            a, *bys = ins
+            total, blocks = scratch
+
+            @pl.when(lax.rem(i, steps) == 0)
+            def _():
+                total[...] = jnp.zeros_like(total)
+
+            def add(by):
+                left = a[...].T
+                for at in range(0, width, 256 if width % CHUNK else CHUNK):
+                    cut = pl.ds(at, 256 if width % CHUNK else CHUNK)
+                    total[:, cut] += dot(left, by[:, cut])
+
+            if len(bys) == 1:
+                add(bys[0])
+            else:
+                pl.when(i < steps)(lambda: add(bys[0]))
+                pl.when(i >= steps)(lambda: add(bys[1]))
+            pl.when(i == steps - 1)(lambda: put_blocks(blocks, total))
+            pl.when(i == 2 * steps - 1)(lambda: put_blocks(outs[0], total))
+
+        if len(bys) == 1:
+            by_specs = [pl.BlockSpec((TOKENS, width), lambda i: (i % steps, i // steps))]
+        else:
+            by_specs = [
+                pl.BlockSpec((TOKENS, width), lambda i: (jnp.minimum(i, steps - 1), 0)),
+                pl.BlockSpec((TOKENS, width), lambda i: (jnp.maximum(i - steps, 0), 0)),
+            ]
+        n_in = 1 + len(bys)
+        body, ins, specs, outs, out_specs, scratch = hidden(compute, n_in, 1, 2, firsts, seconds)
+        return call(
+            body,
+            n_in + len(ins),
+            (2 * steps,),
+            [pl.BlockSpec((TOKENS, m), lambda i: (i % steps, 0)), *by_specs, *specs],
+            [fixed((group, rows, width)), *out_specs],
+            [struct((group, rows, width)), *outs],
+            [pltpu.VMEM((m, width), F32), pltpu.VMEM((group, rows, width), BF16), *scratch],
+            number,
+            4 * tokens * m * width,
+        )(a, *bys, *ins)
+
+    def gate_gradient(by_h, gate, up, a, w_down, number, firsts, seconds):
         tokens, d = a.shape
         ff = gate.shape[1]
-        steps = tokens // ROWS
+        steps = tokens // TOKENS
         rows = d // group
 
         def compute(i, ins, outs, scratch):
@@ -503,70 +555,78 @@
             def _():
                 put_blocks(by_w, total)
 
-        body, ins, specs, outs, out_specs, scratch = hidden(compute, 5, 2, steps, number, first, second)
+        body, ins, specs, outs, out_specs, scratch = hidden(compute, 5, 2, 1, firsts, seconds)
         return call(
             body,
             5 + len(ins),
             (steps,),
-            [tile(ROWS, d), tile(ROWS, ff), tile(ROWS, ff), tile(ROWS, d), whole(w_down.shape), *specs],
-            [tile(ROWS, ff), fixed((group, rows, ff)), *out_specs],
+            [tile(TOKENS, d), tile(TOKENS, ff), tile(TOKENS, ff), tile(TOKENS, d), whole(w_down.shape), *specs],
+            [tile(TOKENS, ff), fixed((group, rows, ff)), *out_specs],
             [struct((tokens, ff)), struct((group, rows, ff)), *outs],
             [pltpu.VMEM((d, ff), F32), *scratch],
             number,
             4 * tokens * d * ff,
         )(by_h, gate, up, a, w_down, *ins)
 
-    def closing(first, second, ready, number):
+    def closing(first, seconds, ready, number):
         half = half_shape(*first.shape[1:])
-        n = len(ready)
+        n, m = len(ready), len(seconds)
 
         def body(ins, outs, scratch):
-            blocks, partial, kept, *ready = ins
-            late, last, squares = outs
+            blocks, *rest = ins
+            *late, last, squares = outs
             spot = Spot(side)
-            greet([spot.near(*way) for way in ((1, 0), (side - 1, 0), (2, 0), (0, 1), (0, side - 1), (0, 2))])
-            ring_1, ring_2, ring_3 = scratch[:13], scratch[13:26], scratch[26:39]
-            partial_2, kept_2, sums, out, came = scratch[39:]
-            one = first_ring(spot, blocks, ring_1, partial_2, kept_2)
-            two = second_ring(spot, partial, kept, ring_2, late)
-            three = second_ring(spot, partial_2, kept_2, ring_3, last)
+            others = [(df, ds) for df in range(side) for ds in range(side) if df or ds]
+            greet([spot.near(*way) for way in others])
+            rings = [scratch[13 * at : 13 * at + 13] for at in range(m + 2)]
+            partial, kept, sums, out, came = scratch[13 * (m + 2) :]
+            one = first_ring(spot, blocks, rings[0], partial, kept)
+            seconds = [second_ring(spot, rest[2 * at], rest[2 * at + 1], rings[1 + at], late[at]) for at in range(m)]
+            final = second_ring(spot, partial, kept, rings[m + 1], last)
             one[0]()
-            two[0]()
-            two[1]()
+            for second in seconds:
+                second[0]()
+            for second in seconds:
+                second[1]()
             one[1]()
-            two[2]()
+            for second in seconds:
+                second[2]()
             total = jnp.zeros((1, 1), F32)
-            for g in [*ready, late]:
+
+            def added(total, g):
                 for h in range(2):
                     wide = g[h].astype(F32)
-                    total += jnp.sum(wide * wide, keepdims=True)
+                    total = total + jnp.sum(wide * wide, keepdims=True)
+                return total
+
+            for g in [*rest[2 * m :], *late]:
+                total = added(total, g)
             one[2]()
-            three[0]()
-            three[1]()
-            three[2]()
-            for h in range(2):
-                wide = last[h].astype(F32)
-                total += jnp.sum(wide * wide, keepdims=True)
-            for axis in range(2):
-                sums[axis, 0] = jnp.broadcast_to(total, sums.shape[2:])
-                for d in range(1, side):
-                    to = spot.near(d, 0) if axis == 0 else spot.near(0, d)
-                    send(sums.at[axis, 0], sums.at[axis, d], out.at[axis, d - 1], came.at[axis, d - 1], dp=to)
-                for d in range(1, side):
-                    await_bytes(sums.at[axis, 0], came.at[axis, d - 1])
-                for d in range(1, side):
-                    total = total + sums[axis, d, 0:1, 0:1]
-                for d in range(1, side):
-                    await_bytes(sums.at[axis, 0], out.at[axis, d - 1])
+            for run in final:
+                run()
+            total = added(total, last)
+            sums[0] = jnp.broadcast_to(total, sums.shape[1:])
+            for at, way in enumerate(others):
+                send(sums.at[0], sums.at[1 + at], out.at[at], came.at[at], dp=spot.near(*way))
+            for at in range(len(others)):
+                await_bytes(sums.at[0], came.at[at])
+                total = total + sums[1 + at, 0:1, 0:1]
             squares[...] = jnp.broadcast_to(total, squares.shape)
+            for at in range(len(others)):
+                await_bytes(sums.at[0], out.at[at])
 
         vmem = pl.BlockSpec(memory_space=pltpu.VMEM)
-        partial, kept = second
-        scratch = ring_scratch(side, half) + ring_scratch(1, half) * 2
-        scratch += [pltpu.VMEM((side, 2, *half), BF16), pltpu.VMEM((2, *half), F32), pltpu.VMEM((2, side, 8, 128), F32)]
-        scratch += [DMA((2, side - 1)), DMA((2, side - 1))]
-        outs = [struct((2, *half)), struct((2, *half)), struct((8, 128), F32)]
-        return call(body, 3 + n, (), [ANY, ANY, vmem] + [vmem] * n, [vmem] * 3, outs, scratch, number, 1000)(first, partial, kept, *ready)
+        scratch = ring_scratch(side, half)
+        for partial, _ in seconds:
+            scratch += ring_scratch(1, partial.shape[2:])
+        scratch += ring_scratch(1, half)
+        scratch += [pltpu.VMEM((side, 2, *half), BF16), pltpu.VMEM((2, *half), F32), pltpu.VMEM((group, 8, 128), F32)]
+        scratch += [DMA((group - 1,)), DMA((group - 1,))]
+        outs = [struct((2, *partial.shape[2:])) for partial, _ in seconds] + [struct((2, *half)), struct((8, 128), F32)]
+        in_specs = [ANY] + [ANY, vmem] * m + [vmem] * n
+        return call(body, 1 + 2 * m + n, (), in_specs, [vmem] * len(outs), outs, scratch, number, 1000)(
+            first, *[one for second in seconds for one in second], *ready
+        )
 
     def adamw(w, m, v, g):
         m = 0.9 * m + 0.1 * g
@@ -575,20 +635,32 @@
         return (w - 0.02 * step).astype(BF16), m, v
 
     def joined(g, shape):
-        return jnp.concatenate([g[0], g[1]], 1 if shape[1] > 1024 else 0)
+        return jnp.concatenate(list(g), 1 if shape[1] > 1024 else 0)
 
     def step(x, dy, *arrays):
         weights, m, v = (arrays[i : i + 3] for i in (0, 3, 6))
+        d, ff = weights[2].shape[2], weights[0].shape[2]
         flat = lambda full: [w.reshape(-1, w.shape[2]) for w in full]
         w_0 = flat(gather_only(weights, 0))
         a_0, gate, up, act, h, *full = forward(x, w_0, weights, 1)
         a_1, by_gate, by_up, by_h, down_1 = last_layer(h, dy, flat(full))
-        gate_1, *down_1 = weight_gradient(a_1, by_gate, 2, down_1, None)
-        up_1, *gate_1, down_1 = weight_gradient(a_1, by_up, 3, gate_1, down_1)
-        down_0, *up_1, gate_1 = weight_gradient(act, by_h, 4, up_1, gate_1)
-        by_up, gate_0, *down_0, up_1 = gate_gradient(by_h, gate, up, a_0, w_0[2], 5, down_0, up_1)
-        up_0, *gate_0, down_0 = weight_gradient(a_0, by_up, 6, gate_0, down_0)
-        gate_0, up_0, squares = closing(up_0, gate_0, [down_1, gate_1, up_1, down_0], 7)
+        shape, cut = (d // group, ff), (d // group, ff // 2)
+        down_shape = (ff // group, d)
+        up_1, *rings = two_gradients(
+            a_1, (by_gate, by_up), ff, 2, [((0, 5, 10), down_1, down_shape), ((8, 13, -1), 1, shape)], []
+        )
+        down_1, gate_1 = rings[:2], rings[2:]
+        down_0, *up_1, down_1, gate_1 = weight_gradient(
+            act, by_h, 3, [((0, 5, -1), up_1, shape)], [((0, 3, 6), down_1), ((1, 4, 7), gate_1)]
+        )
+        by_up, gate_0, *down_0, up_1 = gate_gradient(
+            by_h, gate, up, a_0, w_0[2], 4, [((0, 3, 5), down_0, down_shape)], [((0, 2, 4), up_1)]
+        )
+        up_0b, *rings, down_0 = two_gradients(
+            a_0, (by_up,), ff // 2, 5, [((0, 9, 13), gate_0, shape), ((9, 13, -1), 1, cut)], [((0, 4, 8), down_0)]
+        )
+        gate_0, up_0a, up_0b, squares = closing(up_0b, [rings[:2], rings[2:]], [down_1, gate_1, up_1, down_0], 6)
+        up_0 = jnp.concatenate([up_0a, up_0b], 0)
         count = group * sum(w.size for w in weights)
         factor = jnp.minimum(1.0, 0.5 * lax.rsqrt(squares[0, 0] / count + 1e-30))
         pairs = ((gate_0, gate_1), (up_0, up_1), (down_0, down_1))

time: 564 us -> 553 us (0.980)
  Pallas kernels: 543 us -> 532 us
    pallas_call x4 -> x1, Pallas kernels: 128 us -> 37.2 us  [weight_gradient(): call(body, 2 + len(ins), (steps,), [tile(TOKENS, m), tile(TOKENS, n), *sp...]
    pallas_call x2 -> x4, Pallas kernels: 123 us -> 203 us  [the longest x2 97.9 us: two_gradients(): call(body, n_in + len(ins), (2 * steps,), [pl.BlockSpec((TOKENS, m), lamb...]
where the time goes in v2:
time: 553 us; the launch traced here: 546 us
  Pallas kernels  532 us (96%)
  local copies, waits for them, and re-layouts  6.66 us (1%)
  other arithmetic  5.86 us (1%)
    pallas_call x1, Pallas kernels, last_layer(): call(body, 5, (steps,), in_specs, out_specs, outs, scratch, None, 12 * to...  157 us
    pallas_call x2, Pallas kernels, two_gradients(): call(body, n_in + len(ins), (2 * steps,), [pl.BlockSpec((TOKENS, m), lamb...  97.9 us
    pallas_call x1, Pallas kernels, forward(): call(body, 7, (steps,), in_specs, out_specs, outs, scratch, 1, 6 * tokens...  88.5 us
    pallas_call x1, Pallas kernels, gate_gradient(): call(body, 5 + len(ins), (steps,), [tile(TOKENS, d), tile(TOKENS, ff), ti...  67.8 us
    pallas_call x1, Pallas kernels, gather_only(): call(body, 3, (), [ANY] * 3, [ANY] * 3, outs, scratch, 0, 1000)(*shards)  46.1 us
    pallas_call x1, Pallas kernels, weight_gradient(): call(body, 2 + len(ins), (steps,), [tile(TOKENS, m), tile(TOKENS, n), *sp...  37.2 us
    pallas_call x1, Pallas kernels, closing(): call(body, 1 + 2 * m + n, (), in_specs, [vmem] * len(outs), outs, scratch...  37.1 us

profile of v2, /device:TPU:96, one launch (start us, length us, event | category | flops | bytes accessed | tf_op | source)
XLA Modules:
  0.0 546.4 jit_solution(11325362631381044388)
XLA Ops:
  0.6 46.1 %shard_map.178 = (bf16[16,56,2560]{2,1,0:T(8,128)(2,1)}, bf16[16,56,2560]{2,1,0:T(8,128)(2,1)}, bf16[16,160,896]{2,1,0:T(8,128)(2,1)}) custom-call(bf16[2,56,2560]{2,1,0:T(8,128)(2,1)} %refs_4_.1, bf16[2,56,2560]{2,1,0:T(8,128)(2,1)} %refs_5_.1, bf16[2,160,896]{2,1,0:T(8,128)(2,1)} %refs_6_.1), custom_call_target="tpu_custom_call" | custom-call | flops 1000 | bytes 2 | tf_op jit(solution)/shard_map/pallas_call | solution.py:315
  46.7 88.5 %shard_map.179 = (bf16[4096,896]{1,0:T(8,128)(2,1)}, f32[4096,2560]{1,0:T(8,128)}, f32[4096,2560]{1,0:T(8,128)}, bf16[4096,2560]{1,0:T(8,128)(2,1)}, bf16[4096,8...) custom-call(bf16[1,4096,896]{2,1,0:T(8,128)(2,1)} %refs_0_.3, ...), custom_call_target="tpu_custom_call" | custom-call | flops 56371445760 | bytes 140928608 | tf_op jit(solution)/shard_map/pallas_call | solution.py:357
  135.2 157.2 %shard_map.180 = (bf16[4096,896]{1,0:T(8,128)(2,1)}, bf16[4096,2560]{1,0:T(8,128)(2,1)}, bf16[4096,2560]{1,0:T(8,128)(2,1)}, bf16[4096,896]{1,0:T(8,128)(2,1)}, bf16[16,160,896]{2,1,0:T(8,128)(2,1)}) custom-call(bf16[4096,896]{1,0:T(8,128)(2,1)} %get-tuple-element.54.refs_0_, bf16[1,4096,896]{2,1,0:T(8,128)(2,1)} %refs_1_.3, bf16[896,2560]{1,0:T(8,128)(2,1)} %bitcast.51, ...), custom_call_target="tpu_custom_call" | custom-call | flops 112742891520 | bytes 281857216 | tf_op jit(solution)/shard_map/pallas_call | solution.py:401
  292.5 56.9 %shard_map.181 = (bf16[16,56,2560]{2,1,0:T(8,128)(2,1)}, bf16[4,2,80,896]{3,2,1,0:T(8,128)(2,1)}, f32[2,80,896]{2,1,0:T(8,128)}, bf16[4,2,56,1280]{3,2,1,0:T(8,128)(2,1)}, f32[2,56,1280]{2,1,0:T(8,128)}) custom-call(bf16[4096,896]{1,0:T(8,128)(2,1)} %get-tuple-element.62.refs_0_, bf16[4096,2560]{1,0:T(8,128)(2,1)} %get-tuple-element.63.refs_1_, ...), custom_call_target="tpu_custom_call" | custom-call | flops 37580963840 | bytes 93952408 | tf_op jit(solution)/shard_map/pallas_call | solution.py:521
  349.4 37.2 %shard_map.182 = (bf16[16,160,896]{2,1,0:T(8,128)(2,1)}, bf16[4,2,56,1280]{3,2,1,0:T(8,128)(2,1)}, f32[2,56,1280]{2,1,0:T(8,128)}, bf16[2,80,896]{2,1,0:T(8,128)(2,1)}, bf16[2,56,1280]{2,1,0:T(8,128)(2,1)}) custom-call(bf16[4096,2560]{1,0:T(8,128)(2,1)} %get-tuple-element.61.refs_0_, bf16[4096,896]{1,0:T(8,128)(2,1)} %get-tuple-element.58.refs_1_.refs_0_, ...), custom_call_target="tpu_custom_call" | custom-call | flops 18790481920 | bytes 46976204 | tf_op jit(solution)/shard_map/pallas_call | solution.py:473
  386.6 67.8 %shard_map.183 = (bf16[4096,2560]{1,0:T(8,128)(2,1)}, bf16[16,56,2560]{2,1,0:T(8,128)(2,1)}, bf16[4,2,80,896]{3,2,1,0:T(8,128)(2,1)}, f32[2,80,896]{2,1,0:T(8,128)}, bf16[2,56,1280]{2,1,0:T(8,128)(2,1)}) custom-call(bf16[4096,896]{1,0:T(8,128)(2,1)} %get-tuple-element.58.refs_1_.refs_0_, f32[4096,2560]{1,0:T(8,128)} %get-tuple-element.59.refs_1_, ...), custom_call_target="tpu_custom_call" | custom-call | flops 37580963840 | bytes 93952408 | tf_op jit(solution)/shard_map/pallas_call | solution.py:559
  454.4 41.0 %shard_map.184 = (bf16[16,56,1280]{2,1,0:T(8,128)(2,1)}, bf16[4,2,56,1280]{3,2,1,0:T(8,128)(2,1)}, f32[2,56,1280]{2,1,0:T(8,128)}, bf16[4,2,56,640]{3,2,1,0:T(8,...) custom-call(bf16[4096,896]{1,0:T(8,128)(2,1)} %get-tuple-element.53.refs_3_.refs_0_, ...), custom_call_target="tpu_custom_call" | custom-call | flops 18790481920 | bytes 46976204 | tf_op jit(solution)/shard_map/pallas_call | solution.py:521
  495.4 0.0 copy-start.12
  495.4 37.1 %shard_map.185 = (bf16[2,56,1280]{2,1,0:T(8,128)(2,1)}, bf16[2,56,640]{2,1,0:T(8,128)(2,1)}, bf16[2,56,640]{2,1,0:T(8,128)(2,1)}, f32[8,128]{1,0:T(8,128)}) custom-call(bf16[16,56,1280]{2,1,0:T(8,128)(2,1)} %get-tuple-element.78.refs_0_, bf16[4,2,56,1280]{3,2,1,0:T(8,128)(2,1)} %get-tuple-element.79.refs_1_, f32[2,56,1280]{2,1,0:T(8,128)} %get-tuple-element.80.refs_2_, ...), custom_call_target="tpu_custom_call" | custom-call | flops 1000 | bytes 2 | tf_op jit(solution)/shard_map/pallas_call | solution.py:627
  532.5 0.0 copy-start.11
  532.5 1.2 slice.3
  534.4 0.0 copy-start.10
  534.5 1.0 slice_bitcast_fusion.9
  535.5 0.0 copy-done.12
  535.5 0.0 copy-done.11
  535.6 0.0 copy-start.9
  535.6 0.0 copy-done.10
  535.7 0.0 copy-start.13
  535.7 0.0 copy-start.14
  535.7 0.8 copy-done.9
  536.5 0.0 copy-start.4
  536.6 0.0 copy-start
  536.6 0.0 copy-start.3
  536.6 0.1 maximum_bitcast_fusion.4
  536.7 0.0 copy-done.13
  536.7 0.0 copy-done.14
  536.8 1.1 copy-done.4
  537.8 0.1 copy-done
  538.0 0.4 copy-done.3
  538.3 0.0 copy-start.1
  538.3 0.0 copy-start.5
  538.3 0.0 copy-start.6
  538.3 1.9 fusion.5
  540.3 0.0 copy-done.1
  540.3 0.1 copy-done.5
  540.3 0.8 copy-done.6
  541.2 0.0 copy-start.2
  541.2 0.0 copy-start.7
  541.2 0.0 copy-start.8
  541.2 1.9 fusion.8
  543.1 0.0 copy-done.2
  543.1 0.2 copy-done.7
  543.2 0.7 copy-done.8
  544.0 1.9 fusion.2
  (8 shorter events, 0.2 us)
Async XLA Ops:
  495.4 40.1 %copy-start.12 = (bf16[2,80,896]{2,1,0:T(8,128)(2,1)S(1)}, bf16[2,80,896]{2,1,0:T(8,128)(2,1)}, u32[]{:S(2)}) copy-start(bf16[2,80,896]{2,1,0:T(8,128)(2,1)} %get-tuple-element.86.refs_8_) | copy-start | bytes 860164
  532.5 3.0 copy-start.11
  534.4 1.2 copy-start.10
  535.6 1.0 copy-start.9
  535.7 1.0 copy-start.13
  535.7 1.0 copy-start.14
  536.5 1.3 copy-start.4
  536.6 1.4 copy-start
  536.6 1.8 copy-start.3
  538.3 1.9 copy-start.1
  538.3 2.0 copy-start.5
  538.3 2.8 copy-start.6
  541.2 1.9 copy-start.2
  541.2 2.1 copy-start.7
  541.2 2.8 copy-start.8

commit v3 on v2

--- a/solution.py
+++ b/solution.py
@@ -11,8 +11,8 @@
 F32, BF16 = jnp.float32, jnp.bfloat16
 ANY = pl.BlockSpec(memory_space=pl.ANY)
 DMA = pltpu.SemaphoreType.DMA
-CHUNK = 512
-ROWS, TOKENS = 256, 512
+CHUNK, FINE, COARSE = 512, 256, 1280
+ROWS, TOKENS = 512, 512
 
 
 class Spot:
@@ -176,7 +176,8 @@
 
 
 def ring_scratch(n, half):
-    return [pltpu.VMEM((n, *half), BF16)] * 10 + [DMA((4,)), DMA((6,)), DMA((6,))]
+    here = (n, *half) if n > 1 else (1, 16, 128)
+    return [pltpu.VMEM((n, *half), BF16)] * 4 + [pltpu.VMEM(here, BF16)] * 2 + [pltpu.VMEM((n, *half), BF16)] * 4 + [DMA((4,)), DMA((6,)), DMA((6,))]
 
 
 def ring_stages(source, place, side, plus, minus, scratch, own, done):
@@ -265,8 +266,8 @@
     return silu, (by_act * up * (s + silu * (1 - s))).astype(BF16), (by_act * silu).astype(BF16)
 
 
-def cuts(n):
-    return [pl.ds(at, CHUNK) for at in range(0, n, CHUNK)]
+def cuts(n, width=CHUNK):
+    return [pl.ds(at, width) for at in range(0, n, width)]
 
 
 def put_blocks(out, total):
@@ -326,7 +327,7 @@
             i = pl.program_id(0)
             spot = Spot(side)
             stages = [gather_stages(spot, shards[j], layer, full[j], scratch[4 * j : 4 * j + 4]) for j in range(3)]
-            for number, when in enumerate((0, 2, 4, 9, 12)):
+            for number, when in enumerate((0, 1, 2, 5, 6)):
 
                 @pl.when(i == when)
                 def _():
@@ -377,7 +378,7 @@
             a = (wide * scale).astype(BF16)
             a_out[...] = a
             by_y = dy[...]
-            for cut in cuts(ff):
+            for cut in cuts(ff, FINE):
                 gate, up = dot(a, w_gate[:, cut]), dot(a, w_up[:, cut])
                 by_act = dot_t(by_y, w_down[cut, :]).astype(BF16).astype(F32)
                 silu, by_gate[:, cut], by_up[:, cut] = gated_back(gate, up, by_act)
@@ -387,7 +388,7 @@
             inner = jnp.sum(by_a * wide, -1, keepdims=True) * (scale * scale * scale) * (1 / d)
             by_x = (by_a * scale - wide * inner).astype(BF16)
             by_h[...] = (by_y.astype(F32) + by_x.astype(F32)).astype(BF16)
-            for cut in cuts(ff):
+            for cut in cuts(ff, FINE):
                 total[cut, :] += dot(act[:, cut].T, by_y)
 
             @pl.when(i == steps - 1)
@@ -410,10 +411,14 @@
             more_out += [struct((side, 2, *half)), struct((2, *half), F32)]
             more_out_specs += [fixed((side, 2, *half)), fixed((2, *half))]
             more_scratch += ring_scratch(side, half)
-        for _, (partial, kept) in seconds:
-            half = partial.shape[2:]
-            more_in += [partial, kept]
-            more_specs += [ANY, whole(kept.shape)]
+        for _, second in seconds:
+            if isinstance(second, int):
+                half = half_shape(*firsts[second][2])
+            else:
+                partial, kept = second
+                half = partial.shape[2:]
+                more_in += [partial, kept]
+                more_specs += [ANY, whole(kept.shape)]
             more_out += [struct((2, *half))]
             more_out_specs += [fixed((2, *half))]
             more_scratch += ring_scratch(1, half)
@@ -423,13 +428,16 @@
             spot = Spot(side)
             ins_left, outs_left, rings = list(ins[n_in:]), list(outs[n_out:]), list(scratch[n_scratch:])
             plan = []
+            partials = []
             for when, blocks, _ in firsts:
                 source = scratch[blocks] if isinstance(blocks, int) else ins_left.pop(0)
-                stages = first_ring(spot, source, rings[:13], outs_left.pop(0), outs_left.pop(0))
+                partials.append((outs_left.pop(0), outs_left.pop(0)))
+                stages = first_ring(spot, source, rings[:13], *partials[-1])
                 del rings[:13]
                 plan += list(zip(when, stages, strict=True))
-            for when, _ in seconds:
-                stages = second_ring(spot, ins_left.pop(0), ins_left.pop(0), rings[:13], outs_left.pop(0))
+            for when, second in seconds:
+                partial, kept = partials[second] if isinstance(second, int) else (ins_left.pop(0), ins_left.pop(0))
+                stages = second_ring(spot, partial, kept, rings[:13], outs_left.pop(0))
                 del rings[:13]
                 plan += list(zip(when, stages, strict=True))
 
@@ -497,8 +505,7 @@
 
             def add(by):
                 left = a[...].T
-                for at in range(0, width, 256 if width % CHUNK else CHUNK):
-                    cut = pl.ds(at, 256 if width % CHUNK else CHUNK)
+                for cut in cuts(width, FINE if width % CHUNK else CHUNK):
                     total[:, cut] += dot(left, by[:, cut])
 
             if len(bys) == 1:
@@ -546,7 +553,7 @@
                 total[...] = jnp.zeros_like(total)
 
             by_y, left = by_h[...], a[...].T
-            for cut in cuts(ff):
+            for cut in cuts(ff, COARSE):
                 by_act = dot_t(by_y, w_down[cut, :]).astype(BF16).astype(F32)
                 _, by_gate, by_up[:, cut] = gated_back(gate[:, cut], up[:, cut], by_act)
                 total[:, cut] += dot(left, by_gate)
@@ -568,13 +575,13 @@
             4 * tokens * d * ff,
         )(by_h, gate, up, a, w_down, *ins)
 
-    def closing(first, seconds, ready, number):
+    def closing(first, seconds, ready, count, number):
         half = half_shape(*first.shape[1:])
         n, m = len(ready), len(seconds)
 
         def body(ins, outs, scratch):
             blocks, *rest = ins
-            *late, last, squares = outs
+            *late, last, factor = outs
             spot = Spot(side)
             others = [(df, ds) for df in range(side) for ds in range(side) if df or ds]
             greet([spot.near(*way) for way in others])
@@ -611,7 +618,7 @@
             for at in range(len(others)):
                 await_bytes(sums.at[0], came.at[at])
                 total = total + sums[1 + at, 0:1, 0:1]
-            squares[...] = jnp.broadcast_to(total, squares.shape)
+            factor[...] = jnp.minimum(1.0, 0.5 * lax.rsqrt(total / count + 1e-30))
             for at in range(len(others)):
                 await_bytes(sums.at[0], out.at[at])
 
@@ -622,7 +629,7 @@
         scratch += ring_scratch(1, half)
         scratch += [pltpu.VMEM((side, 2, *half), BF16), pltpu.VMEM((2, *half), F32), pltpu.VMEM((group, 8, 128), F32)]
         scratch += [DMA((group - 1,)), DMA((group - 1,))]
-        outs = [struct((2, *partial.shape[2:])) for partial, _ in seconds] + [struct((2, *half)), struct((8, 128), F32)]
+        outs = [struct((2, *partial.shape[2:])) for partial, _ in seconds] + [struct((2, *half)), struct((1, 1), F32)]
         in_specs = [ANY] + [ANY, vmem] * m + [vmem] * n
         return call(body, 1 + 2 * m + n, (), in_specs, [vmem] * len(outs), outs, scratch, number, 1000)(
             first, *[one for second in seconds for one in second], *ready
@@ -647,22 +654,19 @@
         shape, cut = (d // group, ff), (d // group, ff // 2)
         down_shape = (ff // group, d)
         up_1, *rings = two_gradients(
-            a_1, (by_gate, by_up), ff, 2, [((0, 5, 10), down_1, down_shape), ((8, 13, -1), 1, shape)], []
+            a_1, (by_gate, by_up), ff, 2, [((0, 5, 9), down_1, down_shape), ((8, 13, -1), 1, shape)], []
         )
         down_1, gate_1 = rings[:2], rings[2:]
-        down_0, *up_1, down_1, gate_1 = weight_gradient(
-            act, by_h, 3, [((0, 5, -1), up_1, shape)], [((0, 3, 6), down_1), ((1, 4, 7), gate_1)]
+        down_0, *up_1, down_1 = weight_gradient(act, by_h, 3, [((0, 5, -1), up_1, shape)], [((0, 3, 5), down_1)])
+        by_up, gate_0, _, _, gate_1, up_1, down_0 = gate_gradient(
+            by_h, gate, up, a_0, w_0[2], 4,
+            [((0, 2, 3), down_0, down_shape)],
+            [((0, 1, 2), gate_1), ((0, 1, 3), up_1), ((3, 4, 6), 0)],
         )
-        by_up, gate_0, *down_0, up_1 = gate_gradient(
-            by_h, gate, up, a_0, w_0[2], 4, [((0, 3, 5), down_0, down_shape)], [((0, 2, 4), up_1)]
-        )
-        up_0b, *rings, down_0 = two_gradients(
-            a_0, (by_up,), ff // 2, 5, [((0, 9, 13), gate_0, shape), ((9, 13, -1), 1, cut)], [((0, 4, 8), down_0)]
-        )
-        gate_0, up_0a, up_0b, squares = closing(up_0b, [rings[:2], rings[2:]], [down_1, gate_1, up_1, down_0], 6)
+        up_0b, *rings = two_gradients(a_0, (by_up,), ff // 2, 5, [((0, 9, 13), gate_0, shape), ((8, 13, -1), 1, cut)], [])
+        count = group * sum(w.size for w in weights)
+        gate_0, up_0a, up_0b, factor = closing(up_0b, [rings[:2], rings[2:]], [down_1, gate_1, up_1, down_0], count, 6)
         up_0 = jnp.concatenate([up_0a, up_0b], 0)
-        count = group * sum(w.size for w in weights)
-        factor = jnp.minimum(1.0, 0.5 * lax.rsqrt(squares[0, 0] / count + 1e-30))
         pairs = ((gate_0, gate_1), (up_0, up_1), (down_0, down_1))
         new = []
         for w, m_w, v_w, pair in zip(weights, m, v, pairs, strict=True):

time: 553 us -> 558 us (level)
  no operation moved by 1% of the time
where the time goes in v3:
time: 558 us; the launch traced here: 549 us
  Pallas kernels  537 us (96%)
  other arithmetic  8.24 us (1%)
    pallas_call x1, Pallas kernels, last_layer(): call(body, 5, (steps,), in_specs, out_specs, outs, scratch, None, 12 * to...  159 us
    pallas_call x2, Pallas kernels, two_gradients(): call(body, n_in + len(ins), (2 * steps,), [pl.BlockSpec((TOKENS, m), lamb...  98.3 us
    pallas_call x1, Pallas kernels, forward(): call(body, 7, (steps,), in_specs, out_specs, outs, scratch, 1, 6 * tokens...  90.9 us
    pallas_call x1, Pallas kernels, gate_gradient(): call(body, 5 + len(ins), (steps,), [tile(TOKENS, d), tile(TOKENS, ff), ti...  72.9 us
    pallas_call x1, Pallas kernels, gather_only(): call(body, 3, (), [ANY] * 3, [ANY] * 3, outs, scratch, 0, 1000)(*shards)  46.1 us
    pallas_call x1, Pallas kernels, closing(): call(body, 1 + 2 * m + n, (), in_specs, [vmem] * len(outs), outs, scratch...  36.8 us
    pallas_call x1, Pallas kernels, weight_gradient(): call(body, 2 + len(ins), (steps,), [tile(TOKENS, m), tile(TOKENS, n), *sp...  33.4 us

profile of v3, /device:TPU:96, one launch (start us, length us, event | category | flops | bytes accessed | tf_op | source)
XLA Modules:
  0.0 549.5 jit_solution(319284733264841538)
XLA Ops:
  0.6 46.1 %shard_map.178 = (bf16[16,56,2560]{2,1,0:T(8,128)(2,1)}, bf16[16,56,2560]{2,1,0:T(8,128)(2,1)}, bf16[16,160,896]{2,1,0:T(8,128)(2,1)}) custom-call(bf16[2,56,2560]{2,1,0:T(8,128)(2,1)} %refs_4_.1, bf16[2,56,2560]{2,1,0:T(8,128)(2,1)} %refs_5_.1, bf16[2,160,896]{2,1,0:T(8,128)(2,1)} %refs_6_.1), custom_call_target="tpu_custom_call" | custom-call | flops 1000 | bytes 2 | tf_op jit(solution)/shard_map/pallas_call | solution.py:316
  46.7 90.9 %shard_map.179 = (bf16[4096,896]{1,0:T(8,128)(2,1)}, f32[4096,2560]{1,0:T(8,128)}, f32[4096,2560]{1,0:T(8,128)}, bf16[4096,2560]{1,0:T(8,128)(2,1)}, bf16[4096,8...) custom-call(bf16[1,4096,896]{2,1,0:T(8,128)(2,1)} %refs_0_.3, ...), custom_call_target="tpu_custom_call" | custom-call | flops 56371445760 | bytes 140928608 | tf_op jit(solution)/shard_map/pallas_call | solution.py:358
  137.7 158.8 %shard_map.180 = (bf16[4096,896]{1,0:T(8,128)(2,1)}, bf16[4096,2560]{1,0:T(8,128)(2,1)}, bf16[4096,2560]{1,0:T(8,128)(2,1)}, bf16[4096,896]{1,0:T(8,128)(2,1)}, bf16[16,160,896]{2,1,0:T(8,128)(2,1)}) custom-call(bf16[4096,896]{1,0:T(8,128)(2,1)} %get-tuple-element.52.refs_0_, bf16[1,4096,896]{2,1,0:T(8,128)(2,1)} %refs_1_.3, bf16[896,2560]{1,0:T(8,128)(2,1)} %bitcast.51, ...), custom_call_target="tpu_custom_call" | custom-call | flops 112742891520 | bytes 281857216 | tf_op jit(solution)/shard_map/pallas_call | solution.py:402
  296.4 56.9 %shard_map.181 = (bf16[16,56,2560]{2,1,0:T(8,128)(2,1)}, bf16[4,2,80,896]{3,2,1,0:T(8,128)(2,1)}, f32[2,80,896]{2,1,0:T(8,128)}, bf16[4,2,56,1280]{3,2,1,0:T(8,128)(2,1)}, f32[2,56,1280]{2,1,0:T(8,128)}) custom-call(bf16[4096,896]{1,0:T(8,128)(2,1)} %get-tuple-element.60.refs_0_, bf16[4096,2560]{1,0:T(8,128)(2,1)} %get-tuple-element.61.refs_1_, ...), custom_call_target="tpu_custom_call" | custom-call | flops 37580963840 | bytes 93952408 | tf_op jit(solution)/shard_map/pallas_call | solution.py:528
  353.3 33.4 %shard_map.182 = (bf16[16,160,896]{2,1,0:T(8,128)(2,1)}, bf16[4,2,56,1280]{3,2,1,0:T(8,128)(2,1)}, f32[2,56,1280]{2,1,0:T(8,128)}, bf16[2,80,896]{2,1,0:T(8,128)(2,1)}) custom-call(bf16[4096,2560]{1,0:T(8,128)(2,1)} %get-tuple-element.59.refs_0_, bf16[4096,896]{1,0:T(8,128)(2,1)} %get-tuple-element.56.refs_1_.refs_0_, ...), custom_call_target="tpu_custom_call" | custom-call | flops 18790481920 | bytes 46976204 | tf_op jit(solution)/shard_map/pallas_call | solution.py:481
  386.7 72.9 %shard_map.183 = (bf16[4096,2560]{1,0:T(8,128)(2,1)}, bf16[16,56,2560]{2,1,0:T(8,128)(2,1)}, bf16[4,2,80,896]{3,2,1,0:T(8,128)(2,1)}, f32[2,80,896]{2,1,0:T(8,12...) custom-call(bf16[4096,896]{1,0:T(8,128)(2,1)} %get-tuple-element.56.refs_1_.refs_0_, ...), custom_call_target="tpu_custom_call" | custom-call | flops 37580963840 | bytes 93952408 | tf_op jit(solution)/shard_map/pallas_call | solution.py:566
  459.6 41.4 %shard_map.184 = (bf16[16,56,1280]{2,1,0:T(8,128)(2,1)}, bf16[4,2,56,1280]{3,2,1,0:T(8,128)(2,1)}, f32[2,56,1280]{2,1,0:T(8,128)}, bf16[4,2,56,640]{3,2,1,0:T(8,128)(2,1)}, f32[2,56,640]{2,1,0:T(8,128)}) custom-call(bf16[4096,896]{1,0:T(8,128)(2,1)} %get-tuple-element.51.refs_3_.refs_0_, bf16[4096,2560]{1,0:T(8,128)(2,1)} %get-tuple-element.72.refs_1_, ...), custom_call_target="tpu_custom_call" | custom-call | flops 18790481920 | bytes 46976204 | tf_op jit(solution)/shard_map/pallas_call | solution.py:528
  501.0 0.0 copy-start.9
  501.0 0.0 copy-start.10
  501.0 36.8 %shard_map.185 = (bf16[2,56,1280]{2,1,0:T(8,128)(2,1)}, bf16[2,56,640]{2,1,0:T(8,128)(2,1)}, bf16[2,56,640]{2,1,0:T(8,128)(2,1)}, f32[1,1]{1,0:T(1,128)}) custom-call(bf16[16,56,1280]{2,1,0:T(8,128)(2,1)} %get-tuple-element.74.refs_0_, bf16[4,2,56,1280]{3,2,1,0:T(8,128)(2,1)} %get-tuple-element.75.refs_1_, f32[2,56,1280]{2,1,0:T(8,128)} %get-tuple-element.76.refs_2_, ...), custom_call_target="tpu_custom_call" | custom-call | flops 1000 | bytes 2 | tf_op jit(solution)/shard_map/pallas_call | solution.py:634
  537.8 0.0 copy-start.13
  537.8 0.0 copy-done.9
  537.8 0.0 copy-done.10
  537.8 0.1 slice_bitcast_fusion.5
  537.9 0.0 copy-start.12
  537.9 0.0 copy-start.11
  537.9 0.8 copy-done.13
  538.8 0.1 copy-done.12
  538.9 0.1 copy-done.11
  538.9 0.0 copy-start.14
  538.9 0.0 copy-start.15
  539.0 0.0 copy-start.4
  539.0 0.1 maximum_bitcast_fusion.4
  539.0 0.0 copy-start
  539.1 0.0 copy-start.3
  539.1 0.8 copy-done.14
  539.9 0.1 copy-done.15
  540.0 0.4 copy-done.4
  540.4 0.2 copy-done
  540.5 0.4 copy-done.3
  540.9 0.0 copy-start.1
  540.9 0.0 copy-start.5
  540.9 0.0 copy-start.6
  540.9 2.8 fusion.5
  543.7 0.0 copy-done.1
  543.7 0.0 copy-done.5
  543.7 0.0 copy-done.6
  543.7 0.0 copy-start.2
  543.7 0.0 copy-start.7
  543.7 0.0 copy-start.8
  543.7 2.8 fusion.2
  546.5 0.0 copy-done.2
  546.5 0.0 copy-done.7
  546.5 0.0 copy-done.8
  546.5 2.6 fusion.8
  (8 shorter events, 0.2 us)
Async XLA Ops:
  501.0 36.8 %copy-start.9 = (bf16[2,56,1280]{2,1,0:T(8,128)(2,1)S(1)}, bf16[2,56,1280]{2,1,0:T(8,128)(2,1)}, u32[]{:S(2)}) copy-start(bf16[2,56,1280]{2,1,0:T(8,128)(2,1)} %get-tuple-element.80.refs_6_) | copy-start | bytes 860164
  501.0 36.8 %copy-start.10 = (bf16[2,56,1280]{2,1,0:T(8,128)(2,1)S(1)}, bf16[2,56,1280]{2,1,0:T(8,128)(2,1)}, u32[]{:S(2)}) copy-start(bf16[2,56,1280]{2,1,0:T(8,128)(2,1)} %get-tuple-element.81.refs_7_) | copy-start | bytes 860164
  537.8 1.0 copy-start.13
  537.9 1.0 copy-start.12
  537.9 1.1 copy-start.11
  538.9 0.9 copy-start.14
  538.9 1.0 copy-start.15
  539.0 1.4 copy-start.4
  539.0 1.5 copy-start
  539.1 1.8 copy-start.3
  540.9 2.8 copy-start.1
  540.9 2.8 copy-start.5
  540.9 2.8 copy-start.6
  543.7 2.8 copy-start.2
  543.7 2.8 copy-start.7
  543.7 2.8 copy-start.8
